TPU v7x, 8 devices: a whole 2x2x1 slice. The times are simulated.
8 devices in a mesh: dp: 1 (over z), cy: 2 (over y), cx: 4 (over x, core).
Axes of the slice: x: 2, y: 2, z: 1, core: 2. Of those that a mesh axis runs over, the one named last changes fastest.
Arguments:
- q: bfloat16 [1024, 64, 128], P(('dp', 'cy', 'cx'))
- k: bfloat16 [1024, 8, 128], P(('dp', 'cy', 'cx'))
- v: bfloat16 [1024, 8, 128], P(('dp', 'cy', 'cx'))
Outputs:
- output: bfloat16 [1024, 64, 128], P(('dp', 'cy', 'cx'))
All inputs are finite; a program needn't handle non-finite values.
Results may differ from a plain program's by a relative error of at most 0.00331398.
Values are sent between devices in bfloat16 or wider.
A program may use at most 1 GiB of HBM per device.

v0:
```python
import jax
import jax.numpy as jnp
from jax import lax
from jax.sharding import PartitionSpec as P

NEG = -1.0e30


def init_state(c, value_a3, rep, hd):
    return (jnp.full((value_a3, rep, c), NEG, jnp.float32),
            jnp.zeros((value_a3, rep, c), jnp.float32),
            jnp.zeros((value_a3, rep, c, hd), jnp.float32))


def update(state, qc, kc, vc, mask, scale):
    m, l, acc = state
    s = jnp.einsum('qgrd,kgd->grqk', qc, kc, preferred_element_type=jnp.float32) * scale
    if mask is not None:
        s = jnp.where(mask, s, NEG)
    mn = jnp.maximum(m, jnp.max(s, axis=-1))
    p = jnp.exp(s - mn[..., None])
    alpha = jnp.exp(m - mn)
    l = alpha * l + jnp.sum(p, axis=-1)
    pv = jnp.einsum('grqk,kgd->grqd', p.astype(jnp.bfloat16), vc, preferred_element_type=jnp.float32)
    return (mn, l, alpha[..., None] * acc + pv)


def finish(state, c, nh, hd):
    m, l, acc = state
    o = (acc / l[..., None]).astype(jnp.bfloat16)
    return o.transpose(2, 0, 1, 3).reshape(c, nh, hd)


def solution(mesh):
    ncx = mesh.shape['cx']
    n = mesh.shape['cy'] * ncx
    axes = ('cy', 'cx')
    perm = [(i, (i + 1) % n) for i in range(n)]
    spec = P(('dp', 'cy', 'cx'))

    def local(q, k, v):
        t, nh, hd = q.shape
        value_a3 = k.shape[1]
        rep = nh // value_a3
        c = t // 2
        scale = hd ** -0.5
        r = lax.axis_index('cy') * ncx + lax.axis_index('cx')
        qa = q[:c].reshape(c, value_a3, rep, hd)
        qb = q[c:].reshape(c, value_a3, rep, hd)
        tri = jnp.arange(c)[None, :] <= jnp.arange(c)[:, None]
        sa = update(init_state(c, value_a3, rep, hd), qa, k[:c], v[:c], tri, scale)
        sb = update(init_state(c, value_a3, rep, hd), qb, k[:c], v[:c], None, scale)
        sb = update(sb, qb, k[c:], v[c:], tri, scale)
        kb = k
        vb = v
        for hop in range(1, n):
            kb = lax.ppermute(kb, axes, perm)
            vb = lax.ppermute(vb, axes, perm)
            src = (r - hop) % n
            sb = update(sb, qb, kb[:c], vb[:c], None, scale)
            lower = src < r
            qx = jnp.where(lower, qa, qb)
            kx = jnp.where(lower, kb[:c], kb[c:])
            vx = jnp.where(lower, vb[:c], vb[c:])
            sx = tuple(jnp.where(lower, a, b) for a, b in zip(sa, sb))
            sx = update(sx, qx, kx, vx, None, scale)
            sa = tuple(jnp.where(lower, a, b) for a, b in zip(sx, sa))
            sb = tuple(jnp.where(lower, b, a) for a, b in zip(sx, sb))
        return jnp.concatenate([finish(sa, c, nh, hd), finish(sb, c, nh, hd)], axis=0)

    return jax.shard_map(local, mesh=mesh, in_specs=(spec, spec, spec), out_specs=spec, check_vma=False)
```

profile of v0, /device:TPU:0, one launch (start us, length us, event | category | flops | bytes accessed | tf_op | source)
XLA Modules:
  0.0 102.0 jit_solution(16529606209550304848)
XLA Ops:
  0.0 1.7 %copy.4 = bf16[128,8,128]{2,0,1:T(8,128)(2,1)} copy(bf16[128,8,128]{2,1,0:T(8,128)(2,1)} %param.4) | data formatting | bytes 524288 | tf_op args[1]
  3.5 2.6 %collective-permute-start.7 = (bf16[128,8,128]{2,0,1:T(8,128)(2,1)S(1)}, bf16[128,8,128]{2,0,1:T(8,128)(2,1)}, u32[]{:S(2)}, u32[]{:S(2)}) collective-permute-start(bf16[128,8,128]{2,0,1:T(8,128)(2,1)S(1)} %copy.9), channel_id=1, source_target_pairs={{0,1},{1,2},{2,3},{3,4},{4,5},{5,6},{6,7},{7,0}} | collective-permute-start | bytes 786440 | tf_op jit(solution)/shard_map/ppermute | solution.py:58
  6.3 1.7 %fusion.257 = (bf16[64,64,128]{2,1,0:T(8,128)(2,1)S(1)}, bf16[64,64,128]{2,1,0:T(8,128)(2,1)S(1)}) fusion(bf16[128,64,128]{2,1,0:T(8,128)(2,1)} %param.3), kind=kLoop, calls=%fused_computation.387 | loop fusion | bytes 4194304 | tf_op jit(solution)/shard_map/slice | solution.py:48
  9.4 3.4 %fusion.259 = (f32[8,8,64]{2,1,0:T(8,128)S(1)}, f32[8,8,64,64]{2,3,1,0:T(8,128)}) fusion(bf16[64,8,8,128]{3,0,2,1:T(8,128)(2,1)S(1)} %bitcast.730, bf16[128,8,128]{2,0,1:T(8,128)(2,1)} %copy.4, pred[64,64]{0,1:T(8,128)(4,1)S(1)} %iota_compare_fusion), kind=kOutput, calls=%fused_computation.389 | convolution fusion | flops 67891200 | bytes 2248704 | tf_op jit(solution)/shard_map/qgrd,kgd->grqk/dot_general | solution.py:17
  12.8 3.4 %fusion.258 = (f32[8,8,64]{2,1,0:T(8,128)S(1)}, f32[8,8,64,64]{2,3,1,0:T(8,128)}) fusion(bf16[64,8,8,128]{3,0,2,1:T(8,128)(2,1)S(1)} %bitcast.746, bf16[128,8,128]{2,0,1:T(8,128)(2,1)} %copy.4, pred[64,64]{0,1:T(8,128)(4,1)S(1)} %iota_compare_fusion), kind=kOutput, calls=%fused_computation.388 | convolution fusion | flops 67891200 | bytes 2248704 | tf_op jit(solution)/shard_map/qgrd,kgd->grqk/dot_general | solution.py:17
  16.1 2.0 %bitcast_reduce_fusion.14 = (f32[8,8,64]{2,1,0:T(8,128)S(1)}, f32[8,64,64,8]{2,1,3,0:T(8,128)S(1)}) fusion(bf16[64,8,8,128]{3,0,2,1:T(8,128)(2,1)S(1)} %bitcast.731, bf16[128,8,128]{2,0,1:T(8,128)(2,1)} %copy.4), kind=kOutput, calls=%fused_computation.64 | convolution fusion | flops 67629056 | bytes 2244608 | tf_op jit(solution)/shard_map/qgrd,kgd->grqk/dot_general | solution.py:17
  18.3 2.1 %bitcast_reduce_fusion.12 = (f32[8,8,64]{2,1,0:T(8,128)S(1)}, f32[8,64,64,8]{2,1,3,0:T(8,128)S(1)}) fusion(bf16[64,8,8,128]{3,0,2,1:T(8,128)(2,1)S(1)} %bitcast.747, bf16[64,8,8,128]{3,0,2,1:T(8,128)(2,1)S(1)} %bitcast.732, pred[]{:T(512)S(6)} %lt.64, bf16[128,8,128]{2,0,1:T(8,128)(2,1)} %collective-permute-done), kind=kOutput, calls=%fused_computation.57 | convolution fusion | flops 68218880 | bytes 3425280 | tf_op jit(solution)/shard_map/qgrd,kgd->grqk/dot_general | solution.py:17
  20.4 1.6 %collective-permute-start.8 = (bf16[128,8,128]{2,0,1:T(8,128)(2,1)}, bf16[128,8,128]{2,0,1:T(8,128)(2,1)S(1)}, u32[]{:S(2)}, u32[]{:S(2)}) collective-permute-start(bf16[128,8,128]{2,0,1:T(8,128)(2,1)} %collective-permute-done.7), channel_id=1, source_target_pairs={{0,1},{1,2},{2,3},{3,4},{4,5},{5,6},{6,7},{7,0}} | collective-permute-start | bytes 786440 | tf_op jit(solution)/shard_map/ppermute | solution.py:58
  22.0 2.0 %bitcast_reduce_fusion.13 = (f32[8,8,64]{2,1,0:T(8,128)S(1)}, f32[8,64,64,8]{2,1,3,0:T(8,128)S(1)}) fusion(bf16[64,8,8,128]{3,0,2,1:T(8,128)(2,1)S(1)} %bitcast.733, bf16[128,8,128]{2,0,1:T(8,128)(2,1)} %collective-permute-done), kind=kOutput, calls=%fused_computation.60 | convolution fusion | flops 67629056 | bytes 2244608 | tf_op jit(solution)/shard_map/qgrd,kgd->grqk/dot_general | solution.py:17
  32.3 1.4 %fusion.18 = (f32[8,8,64]{2,1,0:T(8,128)S(1)}, f32[8,8,64]{2,1,0:T(8,128)S(1)}) fusion(f32[8,8,64,64]{2,3,1,0:T(8,128)S(1)} %copy-done, f32[8,8,64]{2,1,0:T(8,128)S(1)} %get-tuple-element.69, f32[8,8,64]{2,1,0:T(8,128)S(1)} %get-tuple-element.61, f32[8,64,64,8]{2,1,3,0:T(8,128)S(1)} %get-tuple-element.78), kind=kLoop, calls=%fused_computation.72 | loop fusion | flops 1302528 | bytes 2162688 | tf_op jit(solution)/shard_map/reduce_sum | solution.py:23
  34.5 3.3 %bitcast_add_fusion.13 = f32[64,8,8,128]{3,0,2,1:T(8,128)S(1)} fusion(f32[8,8,64,128]{3,2,1,0:T(8,128)S(1)} %fusion.79, f32[8,8,64,128]{3,2,1,0:T(8,128)S(1)} %fusion.77, f32[8,64,64,8]{2,1,3,0:T(8,128)S(1)} %get-tuple-element.80, f32[8,8,64]{2,1,0:T(8,128)S(1)} %get-tuple-element.62, f32[64,8,8]{0,2,1:T(8,128)S(1)} %get-tuple-element.68, ...), kind=kOutput, calls=%fused_computation.14 | convolution fusion | flops 70516736 | bytes 7536640 | tf_op jit(solution)/shard_map/grqk,kgd->grqd/dot_general | solution.py:24
  39.0 1.3 %collective-permute-done.2 = bf16[128,8,128]{2,0,1:T(8,128)(2,1)S(1)} collective-permute-done((bf16[128,8,128]{2,0,1:T(8,128)(2,1)S(1)}, bf16[128,8,128]{2,0,1:T(8,128)(2,1)S(1)}, u32[]{:S(2)}, u32[]{:S(2)}) %collective-permute-start.2) | collective-permute-done | bytes 262176 | tf_op jit(solution)/shard_map/ppermute | solution.py:57
  41.5 1.7 %collective-permute-done.9 = bf16[128,8,128]{2,0,1:T(8,128)(2,1)S(1)} collective-permute-done((bf16[128,8,128]{2,0,1:T(8,128)(2,1)S(1)}, bf16[128,8,128]{2,0,1:T(8,128)(2,1)S(1)}, u32[]{:S(2)}, u32[]{:S(2)}) %collective-permute-start.9) | collective-permute-done | bytes 262176 | tf_op jit(solution)/shard_map/ppermute | solution.py:58
  44.3 2.7 %collective-permute-done.3 = bf16[128,8,128]{2,0,1:T(8,128)(2,1)S(1)} collective-permute-done((bf16[128,8,128]{2,0,1:T(8,128)(2,1)S(1)}, bf16[128,8,128]{2,0,1:T(8,128)(2,1)S(1)}, u32[]{:S(2)}, u32[]{:S(2)}) %collective-permute-start.3) | collective-permute-done | bytes 262176 | tf_op jit(solution)/shard_map/ppermute | solution.py:57
  52.4 3.0 %bitcast_add_fusion.12 = f32[64,8,8,128]{3,0,2,1:T(8,128)S(1)} fusion(f32[64,8,8,128]{3,0,2,1:T(8,128)S(1)} %bitcast_add_fusion.13, f32[8,8,64,128]{3,2,1,0:T(8,128)S(1)} %fusion.81, f32[8,64,64,8]{2,1,3,0:T(8,128)S(1)} %get-tuple-element.78, f32[8,8,64]{2,1,0:T(8,128)S(1)} %get-tuple-element.61, f32[64,8,8]{0,2,1:T(8,128)S(1)} %get-tuple-element.67, ...), kind=kOutput, calls=%fused_computation.13 | convolution fusion | flops 70057984 | bytes 7652352 | tf_op jit(solution)/shard_map/grqk,kgd->grqd/dot_general | solution.py:24
  55.3 1.3 %bitcast_add_fusion.11 = f32[64,8,8,128]{3,0,2,1:T(8,128)S(1)} fusion(f32[64,8,8,128]{3,0,2,1:T(8,128)S(1)} %bitcast_add_fusion.13, f32[64,8,8,128]{3,0,2,1:T(8,128)S(1)} %bitcast_add_fusion.12, f32[8,64,64,8]{2,1,3,0:T(8,128)S(1)} %get-tuple-element.76, f32[8,8,64]{2,1,0:T(8,128)S(1)} %get-tuple-element.60, f32[64,8,8]{0,2,1:T(8,128)S(1)} %get-tuple-element.38, ...), kind=kOutput, calls=%fused_computation.12 | convolution fusion | flops 69468160 | bytes 8585217 | tf_op jit(solution)/shard_map/grqk,kgd->grqd/dot_general | solution.py:24
  56.7 2.8 %bitcast_add_fusion.9 = f32[64,8,8,128]{3,0,2,1:T(8,128)S(1)} fusion(f32[64,8,8,128]{3,0,2,1:T(8,128)S(1)} %bitcast_add_fusion.11, f32[8,8,64,128]{3,2,1,0:T(8,128)S(1)} %fusion.72, f32[8,64,64,8]{2,1,3,0:T(8,128)S(1)} %get-tuple-element.92, f32[8,8,64]{2,1,0:T(8,128)S(1)} %get-tuple-element.55, f32[64,8,8]{0,2,1:T(8,128)S(1)} %get-tuple-element.34, ...), kind=kOutput, calls=%fused_computation.10 | convolution fusion | flops 72089600 | bytes 12845058 | tf_op jit(solution)/shard_map/grqk,kgd->grqd/dot_general | solution.py:24
  59.5 2.8 %fusion.53 = (f32[64,8,8,128]{3,0,2,1:T(8,128)S(1)}, f32[64,8,8,128]{3,0,2,1:T(8,128)S(1)}, f32[8,8,64,128]{3,2,1,0:T(8,128)S(1)}) fusion(f32[64,8,8,128]{3,0,2,1:T(8,128)S(1)} %bitcast_add_fusion.9, f32[64,8,8]{0,2,1:T(8,128)S(1)} %get-tuple-element.29, pred[]{:T(512)S(6)} %lt.60, f32[8,8,64,128]{3,2,1,0:T(8,128)S(1)} %fusion.72, ...), kind=kOutput, calls=%fused_computation.107 | convolution fusion | flops 73203712 | bytes 18155520 | tf_op jit(solution)/shard_map/grqk,kgd->grqd/dot_general | solution.py:24
  62.3 2.5 %bitcast_add_fusion.7 = f32[64,8,8,128]{3,0,2,1:T(8,128)S(1)} fusion(f32[64,8,8,128]{3,0,2,1:T(8,128)S(1)} %bitcast_add_fusion.9, f32[8,8,64,128]{3,2,1,0:T(8,128)S(1)} %get-tuple-element.93, f32[64,8,8,128]{3,0,2,1:T(8,128)S(1)} %get-tuple-element.57, f32[8,64,64,8]{2,1,3,0:T(8,128)S(1)} %get-tuple-element.88, f32[8,8,64]{2,1,0:T(8,128)S(1)} %get-tuple-element.53, ...), kind=kOutput, calls=%fused_computation.8 | convolution fusion | flops 71041024 | bytes 10715137 | tf_op jit(solution)/shard_map/grqk,kgd->grqd/dot_general | solution.py:24
  66.8 2.8 %collective-permute-start.12 = (bf16[128,8,128]{2,0,1:T(8,128)(2,1)S(1)}, bf16[128,8,128]{2,0,1:T(8,128)(2,1)S(1)}, u32[]{:S(2)}, u32[]{:S(2)}) collective-permute-start(bf16[128,8,128]{2,0,1:T(8,128)(2,1)S(1)} %collective-permute-done.11), channel_id=1, source_target_pairs={{0,1},{1,2},{2,3},{3,4},{4,5},{5,6},{6,7},{7,0}} | collective-permute-start | bytes 786440 | tf_op jit(solution)/shard_map/ppermute | solution.py:58
  70.7 1.4 %collective-permute-done.5 = bf16[128,8,128]{2,0,1:T(8,128)(2,1)S(1)} collective-permute-done((bf16[128,8,128]{2,0,1:T(8,128)(2,1)S(1)}, bf16[128,8,128]{2,0,1:T(8,128)(2,1)S(1)}, u32[]{:S(2)}, u32[]{:S(2)}) %collective-permute-start.5) | collective-permute-done | bytes 262176 | tf_op jit(solution)/shard_map/ppermute | solution.py:57
  73.3 1.6 %collective-permute-done.12 = bf16[128,8,128]{2,0,1:T(8,128)(2,1)S(1)} collective-permute-done((bf16[128,8,128]{2,0,1:T(8,128)(2,1)S(1)}, bf16[128,8,128]{2,0,1:T(8,128)(2,1)S(1)}, u32[]{:S(2)}, u32[]{:S(2)}) %collective-permute-start.12) | collective-permute-done | bytes 262176 | tf_op jit(solution)/shard_map/ppermute | solution.py:58
  76.5 2.3 %collective-permute-done.6 = bf16[128,8,128]{2,0,1:T(8,128)(2,1)S(1)} collective-permute-done((bf16[128,8,128]{2,0,1:T(8,128)(2,1)S(1)}, bf16[128,8,128]{2,0,1:T(8,128)(2,1)S(1)}, u32[]{:S(2)}, u32[]{:S(2)}) %collective-permute-start.6) | collective-permute-done | bytes 262176 | tf_op jit(solution)/shard_map/ppermute | solution.py:57
  82.4 1.3 %fusion.44 = (f32[8,8,64]{2,1,0:T(8,128)S(1)}, f32[8,8,64]{2,1,0:T(8,128)S(1)}) fusion(f32[8,64,64,8]{2,1,3,0:T(8,128)S(1)} %get-tuple-element.101, f32[8,8,64]{2,1,0:T(8,128)S(1)} %get-tuple-element.46, f32[8,8,64]{2,1,0:T(8,128)S(1)} %get-tuple-element.45, f32[8,64,64,8]{2,1,3,0:T(8,128)S(1)} %get-tuple-element.99), kind=kLoop, calls=%fused_computation.98 | loop fusion | flops 1564672 | bytes 2162688 | tf_op jit(solution)/shard_map/reduce_sum | solution.py:23
  83.7 1.3 %fusion.40 = (f32[8,8,64]{2,1,0:T(8,128)S(1)}, f32[8,8,64]{2,1,0:T(8,128)S(1)}) fusion(f32[8,64,64,8]{2,1,3,0:T(8,128)S(1)} %get-tuple-element.105, f32[8,8,64]{2,1,0:T(8,128)S(1)} %get-tuple-element.48, f32[8,8,64]{2,1,0:T(8,128)S(1)} %get-tuple-element.47, f32[8,64,64,8]{2,1,3,0:T(8,128)S(1)} %get-tuple-element.103), kind=kLoop, calls=%fused_computation.94 | loop fusion | flops 1564672 | bytes 2162688 | tf_op jit(solution)/shard_map/reduce_sum | solution.py:23
  85.7 2.2 %bitcast_add_fusion.5 = f32[64,8,8,128]{3,0,2,1:T(8,128)S(1)} fusion(f32[64,8,8,128]{3,0,2,1:T(8,128)S(1)} %bitcast_add_fusion.7, f32[8,8,64,128]{3,2,1,0:T(8,128)S(1)} %fusion.66, f32[64,8,8,128]{3,0,2,1:T(8,128)S(1)} %get-tuple-element.56, f32[8,64,64,8]{2,1,3,0:T(8,128)S(1)} %get-tuple-element.105, f32[8,8,64]{2,1,0:T(8,128)S(1)} %get-tuple-element.48, ...), kind=kOutput, calls=%fused_computation.6 | convolution fusion | flops 71041024 | bytes 10715137 | tf_op jit(solution)/shard_map/grqk,kgd->grqd/dot_general | solution.py:24
  88.0 2.3 %fusion.55 = (f32[64,8,8,128]{3,0,2,1:T(8,128)S(1)}, f32[64,8,8,128]{3,0,2,1:T(8,128)S(1)}, f32[8,8,64,128]{3,2,1,0:T(8,128)S(1)}) fusion(f32[64,8,8,128]{3,0,2,1:T(8,128)S(1)} %bitcast_add_fusion.5, f32[64,8,8]{0,2,1:T(8,128)S(1)} %get-tuple-element.18, pred[]{:T(512)S(6)} %lt.56, f32[64,8,8,128]{3,0,2,1:T(8,128)S(1)} %get-tuple-element.56, ...), kind=kOutput, calls=%fused_computation.109 | convolution fusion | flops 72155136 | bytes 16041472 | tf_op jit(solution)/shard_map/grqk,kgd->grqd/dot_general | solution.py:24
  90.3 2.3 %bitcast_add_fusion.3 = f32[64,8,8,128]{3,0,2,1:T(8,128)S(1)} fusion(f32[64,8,8,128]{3,0,2,1:T(8,128)S(1)} %bitcast_add_fusion.5, f32[8,8,64,128]{3,2,1,0:T(8,128)S(1)} %get-tuple-element.106, f32[64,8,8,128]{3,0,2,1:T(8,128)S(1)} %get-tuple-element.50, f32[8,64,64,8]{2,1,3,0:T(8,128)S(1)} %get-tuple-element.101, f32[8,8,64]{2,1,0:T(8,128)S(1)} %get-tuple-element.46, ...), kind=kOutput, calls=%fused_computation.4 | convolution fusion | flops 71041024 | bytes 10715137 | tf_op jit(solution)/shard_map/grqk,kgd->grqd/dot_general | solution.py:24
  92.6 2.3 %bitcast_add_fusion.1 = f32[64,8,8,128]{3,0,2,1:T(8,128)S(1)} fusion(f32[64,8,8,128]{3,0,2,1:T(8,128)S(1)} %bitcast_add_fusion.3, f32[8,8,64,128]{3,2,1,0:T(8,128)S(1)} %fusion.60, f32[64,8,8,128]{3,0,2,1:T(8,128)S(1)} %get-tuple-element.49, f32[8,64,64,8]{2,1,3,0:T(8,128)S(1)} %get-tuple-element.97, f32[8,8,64]{2,1,0:T(8,128)S(1)} %get-tuple-element.44, ...), kind=kOutput, calls=%fused_computation.2 | convolution fusion | flops 71041024 | bytes 10715137 | tf_op jit(solution)/shard_map/grqk,kgd->grqd/dot_general | solution.py:24
  94.9 2.9 %divide_convert_fusion.1 = (bf16[64,8,8,128]{3,0,2,1:T(8,128)(2,1)S(1)}, f32[64,8,8,128]{3,0,2,1:T(8,128)S(1)}, f32[8,8,64,128]{3,2,1,0:T(8,128)S(1)}) fusion(f32[64,8,8,128]{3,0,2,1:T(8,128)S(1)} %bitcast_add_fusion.1, f32[64,8,8]{0,2,1:T(8,128)S(1)} %get-tuple-element.7, f32[64,8,8]{0,2,1:T(8,128)S(1)} %get-tuple-element.8, pred[]{:T(512)S(6)} %lt.52, ...), kind=kOutput, calls=%fused_computation.68 | convolution fusion | flops 73203712 | bytes 15009280 | tf_op jit(solution)/shard_map/grqk,kgd->grqd/dot_general | solution.py:24
  97.8 1.3 %divide_convert_fusion = bf16[64,8,8,128]{3,0,2,1:T(8,128)(2,1)S(1)} fusion(f32[64,8,8,128]{3,0,2,1:T(8,128)S(1)} %bitcast_add_fusion.1, f32[8,8,64,128]{3,2,1,0:T(8,128)S(1)} %get-tuple-element.107, f32[64,8,8,128]{3,0,2,1:T(8,128)S(1)} %get-tuple-element.6, f32[64,8,8]{0,2,1:T(8,128)S(1)} %broadcast_select_fusion.26, f32[64,8,8]{0,2,1:T(8,128)S(1)} %get-tuple-element.8, ...), kind=kLoop, calls=%fused_computation.67 | loop fusion | flops 3145728 | bytes 7372801 | tf_op jit(solution)/shard_map/convert_element_type | solution.py:30
  100.5 1.5 %pad_maximum_fusion = bf16[128,64,128]{2,1,0:T(8,128)(2,1)} fusion(bf16[64,64,128]{2,1,0:T(8,128)(2,1)S(1)} %copy.30, bf16[64,64,128]{2,1,0:T(8,128)(2,1)S(1)} %copy.29), kind=kLoop, calls=%fused_computation | loop fusion | flops 1048576 | bytes 4194304 | tf_op jit(solution)/shard_map/concatenate | solution.py:69
  (62 shorter events, 32.4 us)
Async XLA Ops:
  1.7 16.5 %collective-permute-start = (bf16[128,8,128]{2,0,1:T(8,128)(2,1)}, bf16[128,8,128]{2,0,1:T(8,128)(2,1)}, u32[]{:S(2)}, u32[]{:S(2)}) collective-permute-start(bf16[128,8,128]{2,0,1:T(8,128)(2,1)} %copy.4), channel_id=1, source_target_pairs={{0,1},{1,2},{2,3},{3,4},{4,5},{5,6},{6,7},{7,0}} | collective-permute-start | bytes 786440 | tf_op jit(solution)/shard_map/ppermute | solution.py:57
  3.5 16.8 %collective-permute-start.7 = (bf16[128,8,128]{2,0,1:T(8,128)(2,1)S(1)}, bf16[128,8,128]{2,0,1:T(8,128)(2,1)}, u32[]{:S(2)}, u32[]{:S(2)}) collective-permute-start(bf16[128,8,128]{2,0,1:T(8,128)(2,1)S(1)} %copy.9), channel_id=1, source_target_pairs={{0,1},{1,2},{2,3},{3,4},{4,5},{5,6},{6,7},{7,0}} | collective-permute-start | bytes 786440 | tf_op jit(solution)/shard_map/ppermute | solution.py:58
  18.2 6.7 %collective-permute-start.1 = (bf16[128,8,128]{2,0,1:T(8,128)(2,1)}, bf16[128,8,128]{2,0,1:T(8,128)(2,1)S(1)}, u32[]{:S(2)}, u32[]{:S(2)}) collective-permute-start(bf16[128,8,128]{2,0,1:T(8,128)(2,1)} %collective-permute-done), channel_id=1, source_target_pairs={{0,1},{1,2},{2,3},{3,4},{4,5},{5,6},{6,7},{7,0}} | collective-permute-start | bytes 786440 | tf_op jit(solution)/shard_map/ppermute | solution.py:57
  20.4 13.4 %collective-permute-start.8 = (bf16[128,8,128]{2,0,1:T(8,128)(2,1)}, bf16[128,8,128]{2,0,1:T(8,128)(2,1)S(1)}, u32[]{:S(2)}, u32[]{:S(2)}) collective-permute-start(bf16[128,8,128]{2,0,1:T(8,128)(2,1)} %collective-permute-done.7), channel_id=1, source_target_pairs={{0,1},{1,2},{2,3},{3,4},{4,5},{5,6},{6,7},{7,0}} | collective-permute-start | bytes 786440 | tf_op jit(solution)/shard_map/ppermute | solution.py:58
  26.1 1.6 %copy-start.1 = (f32[8,8,64,64]{2,3,1,0:T(8,128)S(1)}, f32[8,8,64,64]{2,3,1,0:T(8,128)}, u32[]{:S(2)}) copy-start(f32[8,8,64,64]{2,3,1,0:T(8,128)} %get-tuple-element.82) | copy-start | bytes 3145732
  28.8 1.6 %copy-start = (f32[8,8,64,64]{2,3,1,0:T(8,128)S(1)}, f32[8,8,64,64]{2,3,1,0:T(8,128)}, u32[]{:S(2)}) copy-start(f32[8,8,64,64]{2,3,1,0:T(8,128)} %get-tuple-element.72) | copy-start | bytes 3145732
  33.6 6.7 %collective-permute-start.2 = (bf16[128,8,128]{2,0,1:T(8,128)(2,1)S(1)}, bf16[128,8,128]{2,0,1:T(8,128)(2,1)S(1)}, u32[]{:S(2)}, u32[]{:S(2)}) collective-permute-start(bf16[128,8,128]{2,0,1:T(8,128)(2,1)S(1)} %collective-permute-done.1), channel_id=1, source_target_pairs={{0,1},{1,2},{2,3},{3,4},{4,5},{5,6},{6,7},{7,0}} | collective-permute-start | bytes 786440 | tf_op jit(solution)/shard_map/ppermute | solution.py:57
  33.8 9.4 %collective-permute-start.9 = (bf16[128,8,128]{2,0,1:T(8,128)(2,1)S(1)}, bf16[128,8,128]{2,0,1:T(8,128)(2,1)S(1)}, u32[]{:S(2)}, u32[]{:S(2)}) collective-permute-start(bf16[128,8,128]{2,0,1:T(8,128)(2,1)S(1)} %collective-permute-done.8), channel_id=1, source_target_pairs={{0,1},{1,2},{2,3},{3,4},{4,5},{5,6},{6,7},{7,0}} | collective-permute-start | bytes 786440 | tf_op jit(solution)/shard_map/ppermute | solution.py:58
  40.4 6.7 %collective-permute-start.3 = (bf16[128,8,128]{2,0,1:T(8,128)(2,1)S(1)}, bf16[128,8,128]{2,0,1:T(8,128)(2,1)S(1)}, u32[]{:S(2)}, u32[]{:S(2)}) collective-permute-start(bf16[128,8,128]{2,0,1:T(8,128)(2,1)S(1)} %collective-permute-done.2), channel_id=1, source_target_pairs={{0,1},{1,2},{2,3},{3,4},{4,5},{5,6},{6,7},{7,0}} | collective-permute-start | bytes 786440 | tf_op jit(solution)/shard_map/ppermute | solution.py:57
  43.2 8.9 %collective-permute-start.10 = (bf16[128,8,128]{2,0,1:T(8,128)(2,1)S(1)}, bf16[128,8,128]{2,0,1:T(8,128)(2,1)S(1)}, u32[]{:S(2)}, u32[]{:S(2)}) collective-permute-start(bf16[128,8,128]{2,0,1:T(8,128)(2,1)S(1)} %collective-permute-done.9), channel_id=1, source_target_pairs={{0,1},{1,2},{2,3},{3,4},{4,5},{5,6},{6,7},{7,0}} | collective-permute-start | bytes 786440 | tf_op jit(solution)/shard_map/ppermute | solution.py:58
  51.9 13.4 %collective-permute-start.4 = (bf16[128,8,128]{2,0,1:T(8,128)(2,1)S(1)}, bf16[128,8,128]{2,0,1:T(8,128)(2,1)S(1)}, u32[]{:S(2)}, u32[]{:S(2)}) collective-permute-start(bf16[128,8,128]{2,0,1:T(8,128)(2,1)S(1)} %collective-permute-done.3), channel_id=1, source_target_pairs={{0,1},{1,2},{2,3},{3,4},{4,5},{5,6},{6,7},{7,0}} | collective-permute-start | bytes 786440 | tf_op jit(solution)/shard_map/ppermute | solution.py:57
  52.1 14.7 %collective-permute-start.11 = (bf16[128,8,128]{2,0,1:T(8,128)(2,1)S(1)}, bf16[128,8,128]{2,0,1:T(8,128)(2,1)S(1)}, u32[]{:S(2)}, u32[]{:S(2)}) collective-permute-start(bf16[128,8,128]{2,0,1:T(8,128)(2,1)S(1)} %collective-permute-done.10), channel_id=1, source_target_pairs={{0,1},{1,2},{2,3},{3,4},{4,5},{5,6},{6,7},{7,0}} | collective-permute-start | bytes 786440 | tf_op jit(solution)/shard_map/ppermute | solution.py:58
  65.4 6.7 %collective-permute-start.5 = (bf16[128,8,128]{2,0,1:T(8,128)(2,1)S(1)}, bf16[128,8,128]{2,0,1:T(8,128)(2,1)S(1)}, u32[]{:S(2)}, u32[]{:S(2)}) collective-permute-start(bf16[128,8,128]{2,0,1:T(8,128)(2,1)S(1)} %collective-permute-done.4), channel_id=1, source_target_pairs={{0,1},{1,2},{2,3},{3,4},{4,5},{5,6},{6,7},{7,0}} | collective-permute-start | bytes 786440 | tf_op jit(solution)/shard_map/ppermute | solution.py:57
  66.8 8.2 %collective-permute-start.12 = (bf16[128,8,128]{2,0,1:T(8,128)(2,1)S(1)}, bf16[128,8,128]{2,0,1:T(8,128)(2,1)S(1)}, u32[]{:S(2)}, u32[]{:S(2)}) collective-permute-start(bf16[128,8,128]{2,0,1:T(8,128)(2,1)S(1)} %collective-permute-done.11), channel_id=1, source_target_pairs={{0,1},{1,2},{2,3},{3,4},{4,5},{5,6},{6,7},{7,0}} | collective-permute-start | bytes 786440 | tf_op jit(solution)/shard_map/ppermute | solution.py:58
  72.1 6.7 %collective-permute-start.6 = (bf16[128,8,128]{2,0,1:T(8,128)(2,1)S(1)}, bf16[128,8,128]{2,0,1:T(8,128)(2,1)S(1)}, u32[]{:S(2)}, u32[]{:S(2)}) collective-permute-start(bf16[128,8,128]{2,0,1:T(8,128)(2,1)S(1)} %collective-permute-done.5), channel_id=1, source_target_pairs={{0,1},{1,2},{2,3},{3,4},{4,5},{5,6},{6,7},{7,0}} | collective-permute-start | bytes 786440 | tf_op jit(solution)/shard_map/ppermute | solution.py:57
  74.9 17.7 %collective-permute-start.13 = (bf16[128,8,128]{2,0,1:T(8,128)(2,1)S(1)}, bf16[128,8,128]{2,0,1:T(8,128)(2,1)S(1)}, u32[]{:S(2)}, u32[]{:S(2)}) collective-permute-start(bf16[128,8,128]{2,0,1:T(8,128)(2,1)S(1)} %collective-permute-done.12), channel_id=1, source_target_pairs={{0,1},{1,2},{2,3},{3,4},{4,5},{5,6},{6,7},{7,0}} | collective-permute-start | bytes 786440 | tf_op jit(solution)/shard_map/ppermute | solution.py:58
where the time goes:
time: 103 us; the launch traced here: 102 us
  matrix products  57.9 us (56%)
  other arithmetic  14.1 us (14%)
  waiting for transfers between devices  12 us (12%)
  starting transfers between devices  9.59 us (9%)
  local copies, waits for them, and re-layouts  7.91 us (8%)
    dot_general x17, matrix products, update(): jnp.einsum('grqk,kgd->grqd', p.astype(jnp.bfloat16), vc, preferred_elemen...  31.2 us
    dot_general x17, matrix products, update(): jnp.einsum('qgrd,kgd->grqk', qc, kc, preferred_element_type=jnp.float32)  26.7 us
    reduce_sum x10, other arithmetic, update(): l = alpha * l + jnp.sum(p, axis=-1)  10.8 us
    ppermute x7, waiting for transfers between devices, local(): kb = lax.ppermute(kb, axes, perm)  8.73 us
    ppermute x7, starting transfers between devices, local(): vb = lax.ppermute(vb, axes, perm)  8.41 us
    unnamed x6, local copies, waits for them, and re-layouts  3.47 us
    ppermute x7, waiting for transfers between devices, local(): vb = lax.ppermute(vb, axes, perm)  3.32 us
    slice x2, local copies, waits for them, and re-layouts, local(): qa = q[:c].reshape(c, value_a3, rep, hd)  2.39 us
  transfers between devices with their start and end apart: 14, of which 7 were waited for; matrix products, arithmetic and copies ran while one was open for 67% of the time, Pallas kernels for 0%

commit v1 on v0

v1 whole, which is shorter than its diff:
```python
import functools

import jax
import jax.numpy as jnp
from jax import lax
from jax.experimental import pallas as pl
from jax.experimental.pallas import tpu as pltpu
from jax.sharding import PartitionSpec as P

NEG = -1.0e30
LOG2E = 1.4426950408889634
MESH = pl.DeviceIdType.MESH

SIB, X, Y = 1, 2, 4
LEAD = 4


def attend(qs, keys, vals, biases, c):
    nt = (((1,), (1,)), ((), ()))
    ss = []
    for k, b in zip(keys, biases):
        s = lax.dot_general(qs, k, nt, preferred_element_type=jnp.float32) * c
        ss.append(s if b is None else s + b)
    m = jnp.max(ss[0], axis=-1, keepdims=True)
    for s in ss[1:]:
        m = jnp.maximum(m, jnp.max(s, axis=-1, keepdims=True))
    return ss, m


def weigh(ss, m, vals):
    l = None
    acc = None
    for s, v in zip(ss, vals):
        p = jnp.exp2(s - m)
        pl_ = jnp.sum(p, axis=-1, keepdims=True)
        pv = jnp.dot(p.astype(jnp.bfloat16), v, preferred_element_type=jnp.float32)
        l = pl_ if l is None else l + pl_
        acc = pv if acc is None else acc + pv
    return l, acc


def main_kernel(ncx, scale, q_hbm, k_hbm, v_hbm, o_ref,
                q_s, kv_s, kin, f32s, bias_s, m_s, l_s, acc_s,
                q_sem, in_sem, ss, rs):
    nk, rows = q_s.shape[0], q_s.shape[1]
    c_rows = rows // 2
    rep = q_s.shape[2]
    hd = q_s.shape[3]
    half = c_rows * rep
    icy, icx = lax.axis_index('cy'), lax.axis_index('cx')
    dp = lax.axis_index('dp')
    me = icy * ncx + icx
    c = scale * LOG2E

    def dev(mask):
        t = me ^ mask
        return (dp, t // ncx, t % ncx)

    bar = pltpu.get_barrier_semaphore()
    for mask in (SIB, X, Y):
        pl.semaphore_signal(bar, inc=1, device_id=dev(mask), device_id_type=MESH)

    kcp = pltpu.make_async_copy(k_hbm, kin.at[0], in_sem.at[0])
    vcp = pltpu.make_async_copy(v_hbm, kin.at[1], in_sem.at[1])
    kcp.start()
    vcp.start()

    def qcopy(g):
        return pltpu.make_async_copy(q_hbm.at[:, g], q_s.at[g], q_sem.at[g])

    for g in range(nk):
        qcopy(g).start()

    def rcopy(kind, g, src, dst, mask):
        return pltpu.make_async_remote_copy(
            src_ref=src, dst_ref=dst, send_sem=ss.at[kind, g], recv_sem=rs.at[kind, g],
            device_id=dev(mask), device_id_type=MESH)

    def own(g, kind, mask):
        return rcopy(kind, g, kv_s.at[g, :, :, 0], kv_s.at[g, :, :, mask], mask)

    def own_sib(g):
        return own(g, 0, SIB)

    def own_x(g):
        return own(g, 1, X)

    def own_y(g):
        return own(g, 2, Y)

    def fwd_v(g):
        return rcopy(3, g, kv_s.at[g, 1, :, X], kv_s.at[g, 1, :, X ^ Y], Y)

    def fwd_k(g):
        return rcopy(4, g, kv_s.at[g, 0, :, Y], kv_s.at[g, 0, :, X ^ Y], X)

    def sib_x(g):
        return rcopy(5, g, kv_s.at[g, :, :, X], kv_s.at[g, :, :, X ^ SIB], SIB)

    def sib_y(g):
        return rcopy(6, g, kv_s.at[g, :, :, Y], kv_s.at[g, :, :, Y ^ SIB], SIB)

    def sib_d(g):
        return rcopy(7, g, kv_s.at[g, :, :, X ^ Y], kv_s.at[g, :, :, X ^ Y ^ SIB], SIB)

    shape = (half, 4 * c_rows)
    qi = lax.broadcasted_iota(jnp.int32, shape, 0) // rep
    col = lax.broadcasted_iota(jnp.int32, shape, 1)
    slot = col // c_rows
    kk = col % c_rows
    diag = (slot == 0) & (kk <= qi)
    e = slot ^ me
    bias_s[0] = jnp.where(diag | (e < me), 0.0, NEG)
    bias_s[1] = jnp.where(diag | (e > me), 0.0, NEG)

    kcp.wait()
    vcp.wait()
    for i in range(2):
        f32s[i] = kin[i].astype(jnp.float32).reshape(rows * nk, hd)
    for g in range(nk):
        for i in range(2):
            x = f32s[i, pl.ds(g, rows, stride=nk), :].astype(jnp.bfloat16)
            kv_s[g, i, 0, 0] = x[:c_rows]
            kv_s[g, i, 1, 0] = x[c_rows:]

    pl.semaphore_wait(bar, 3)

    for g in range(nk):
        if g < LEAD:
            own_x(g).start()
            own_y(g).start()
        own_sib(g).start()

    def keys(g, i, fs, far):
        return kv_s[g, i, fs, pl.ds(4 * far, 4)].reshape(4 * c_rows, hd)

    def qrows(g, part):
        return q_s[g, pl.ds(part * c_rows, c_rows)].reshape(half, hd)

    def save(g, part, m, l, acc):
        sl = pl.ds(part * half, half)
        m_s[g, sl, :] = jnp.broadcast_to(m, (half, hd))
        l_s[g, sl, :] = jnp.broadcast_to(l, (half, hd))
        acc_s[g, sl, :] = acc

    def finish(g, part, l, acc):
        o = (acc * (1.0 / l)).astype(jnp.bfloat16)
        o_ref[g, pl.ds(part * c_rows, c_rows)] = o.reshape(c_rows, rep, hd)

    def near(g):
        kf, ks = keys(g, 0, 0, 0), keys(g, 0, 1, 0)
        vf, vs = keys(g, 1, 0, 0), keys(g, 1, 1, 0)
        s, m = attend(qrows(g, 0), [kf], [vf], [bias_s[0]], c)
        l, acc = weigh(s, m, [vf])
        save(g, 0, m, l, acc)
        s, m = attend(qrows(g, 1), [kf, ks], [vf, vs], [None, bias_s[1]], c)
        l, acc = weigh(s, m, [vf, vs])
        save(g, 1, m, l, acc)

    def fold(g, part, kk_, vv):
        sl = pl.ds(part * half, half)
        m0, l0, acc0 = m_s[g, sl, 0:1], l_s[g, sl, 0:1], acc_s[g, sl, :]
        s, m = attend(qrows(g, part), kk_, vv, [None] * len(kk_), c)
        m = jnp.maximum(m, m0)
        l, acc = weigh(s, m, vv)
        al = jnp.exp2(m0 - m)
        finish(g, part, l0 * al + l, acc0 * al + acc)

    def far(g):
        @pl.when(icy == 0)
        def _():
            sl = pl.ds(0, half)
            finish(g, 0, l_s[g, sl, 0:1], acc_s[g, sl, :])
            fold(g, 1, [keys(g, 0, 0, 1), keys(g, 0, 1, 1)], [keys(g, 1, 0, 1), keys(g, 1, 1, 1)])

        @pl.when(icy != 0)
        def _():
            for part in range(2):
                fold(g, part, [keys(g, 0, 0, 1)], [keys(g, 1, 0, 1)])

    def take_diag(g):
        fwd_v(g).wait_recv()
        fwd_k(g).wait_recv()
        sib_d(g).start()

    def step(g, _):
        @pl.when(g < nk)
        def _():
            own_x(g).wait_recv()
            fwd_v(g).start()
            sib_x(g).start()
            own_y(g).wait_recv()
            fwd_k(g).start()
            sib_y(g).start()

            @pl.when(g + LEAD < nk)
            def _():
                own_x(g + LEAD).start()
                own_y(g + LEAD).start()

            qcopy(g).wait()
            own_sib(g).wait_recv()
            sib_x(g).wait_recv()
            near(g)

        @pl.when((g >= LEAD - 1) & (g - LEAD + 1 < nk))
        def _():
            take_diag(g - LEAD + 1)

        @pl.when(g >= LEAD)
        def _():
            h = g - LEAD
            sib_y(h).wait_recv()
            sib_d(h).wait_recv()
            far(h)
        return 0

    lax.fori_loop(0, nk + LEAD, step, 0)

    def drain(g, _):
        for f in (own_sib, own_x, own_y, fwd_v, fwd_k, sib_x, sib_y, sib_d):
            f(g).wait_send()
        return 0

    lax.fori_loop(0, nk, drain, 0)


def store_kernel(o_ref, out, sem):
    cps = [pltpu.make_async_copy(o_ref.at[g], out.at[:, g], sem.at[g]) for g in range(o_ref.shape[0])]
    for cp in cps:
        cp.start()
    for cp in cps:
        cp.wait()


def solution(mesh):
    ncx = mesh.shape['cx']
    spec = P(('dp', 'cy', 'cx'))
    bf16, f32 = jnp.bfloat16, jnp.float32

    def local(q, k, v):
        t, nh, hd = q.shape
        nk = k.shape[1]
        rep = nh // nk
        n = mesh.shape['cy'] * ncx
        c = t // 2
        scale = hd ** -0.5
        q4 = q.reshape(t, nk, rep, hd)
        hbm = pl.BlockSpec(memory_space=pltpu.HBM)
        vmem = pl.BlockSpec(memory_space=pltpu.VMEM)
        o = pl.pallas_call(
            functools.partial(main_kernel, ncx, scale),
            out_shape=pltpu.VMEM((nk, t, rep, hd), bf16),
            in_specs=[hbm, hbm, hbm],
            out_specs=vmem,
            scratch_shapes=[
                pltpu.VMEM((nk, t, rep, hd), bf16),
                pltpu.VMEM((nk, 2, 2, n, c, hd), bf16),
                pltpu.VMEM((2, t, nk, hd), bf16),
                pltpu.VMEM((2, t * nk, hd), f32),
                pltpu.VMEM((2, c * rep, 4 * c), f32),
                pltpu.VMEM((nk, t * rep, hd), f32),
                pltpu.VMEM((nk, t * rep, hd), f32),
                pltpu.VMEM((nk, t * rep, hd), f32),
                pltpu.SemaphoreType.DMA((nk,)),
                pltpu.SemaphoreType.DMA((2,)),
                pltpu.SemaphoreType.DMA((8, nk)),
                pltpu.SemaphoreType.DMA((8, nk)),
            ],
            compiler_params=pltpu.CompilerParams(
                collective_id=0, has_side_effects=True, vmem_limit_bytes=48 * 2**20),
        )(*(pltpu.with_memory_space_constraint(x, pltpu.HBM) for x in (q4, k, v)))
        o = pltpu.with_memory_space_constraint(o, pltpu.VMEM)
        out = pl.pallas_call(
            store_kernel,
            out_shape=jax.ShapeDtypeStruct((t, nk, rep, hd), bf16),
            in_specs=[vmem],
            out_specs=hbm,
            scratch_shapes=[pltpu.SemaphoreType.DMA((nk,))],
            compiler_params=pltpu.CompilerParams(vmem_limit_bytes=2**20),
        )(o)
        return out.reshape(t, nh, hd)

    return jax.shard_map(local, mesh=mesh, in_specs=(spec, spec, spec), out_specs=spec, check_vma=False)
```

time: 103 us -> 45.8 us (0.44)
  the two profiles are of different devices: /device:TPU:0 before, /device:TPU:4 now
where the time goes in v1:
time: 45.8 us; the launch traced here: 45.7 us
  Pallas kernels  45.7 us (100%)
    pallas_call x1, Pallas kernels, local(): pl.pallas_call(functools.partial(main_kernel, ncx, scale), out_shape=pltp...  44.3 us
    pallas_call x1, Pallas kernels, local(): pl.pallas_call(store_kernel, out_shape=jax.ShapeDtypeStruct((t, nk, rep,...  1.38 us

profile of v1, /device:TPU:4, one launch (start us, length us, event | category | flops | bytes accessed | tf_op | source)
XLA Modules:
  0.0 45.7 jit_solution(319639604720446001)
XLA Ops:
  0.0 44.3 %shard_map.37.o_ref = bf16[8,128,8,128]{3,2,1,0:T(8,128)(2,1)S(1)} custom-call(bf16[128,8,8,128]{3,2,1,0:T(8,128)(2,1)} %bitcast.2, bf16[128,8,128]{2,1,0:T(8,128)(2,1)} %k_hbm.1, bf16[128,8,128]{2,1,0:T(8,128)(2,1)} %v_hbm.1), custom_call_target="tpu_custom_call" | custom-call | tf_op jit(solution)/shard_map/pallas_call | solution.py:251
  44.3 1.4 %shard_map.38 = bf16[128,8,8,128]{3,2,1,0:T(8,128)(2,1)} custom-call(bf16[8,128,8,128]{3,2,1,0:T(8,128)(2,1)S(1)} %shard_map.37.o_ref), custom_call_target="tpu_custom_call" | custom-call | tf_op jit(solution)/shard_map/pallas_call | solution.py:274

commit v2 on v1

v2 whole, which is shorter than its diff:
```python
import functools

import jax
import jax.numpy as jnp
from jax import lax
from jax.experimental import pallas as pl
from jax.experimental.pallas import tpu as pltpu
from jax.sharding import PartitionSpec as P

NEG = -1.0e30
LOG2E = 1.4426950408889634
MESH = pl.DeviceIdType.MESH
NT = (((1,), (1,)), ((), ()))
LANES = 128

SIB, X, Y = 1, 2, 4
LEAD = 4


def lane_blocks(s):
    return [s[:, i:i + LANES] for i in range(0, s.shape[1], LANES)]


def tree(f, xs):
    xs = list(xs)
    while len(xs) > 1:
        xs = [f(*xs[i:i + 2]) if i + 1 < len(xs) else xs[i] for i in range(0, len(xs), 2)]
    return xs[0]


def scores(q, k):
    return lax.dot_general(q, k, NT, preferred_element_type=jnp.float32)


def row_max(ss):
    return jnp.max(tree(jnp.maximum, [b for s in ss for b in lane_blocks(s)]), axis=-1, keepdims=True)


def weigh(ss, vals, m, c):
    ls, acc = [], None
    for s, v in zip(ss, vals):
        ps = [jnp.exp2(b * c - m) for b in lane_blocks(s)]
        ls += ps
        p = jnp.concatenate([b.astype(jnp.bfloat16) for b in ps], axis=1)
        pv = jnp.dot(p, v, preferred_element_type=jnp.float32)
        acc = pv if acc is None else acc + pv
    return tree(jnp.add, ls), acc


def normed(l, acc):
    return (acc * (1.0 / jnp.sum(l, axis=-1, keepdims=True))).astype(jnp.bfloat16)


def fold(q, kk, vv, m0, l0, acc0, c):
    ss = [scores(q, k) for k in kk]
    m = jnp.maximum(m0, row_max(ss) * c)
    l, acc = weigh(ss, vv, m, c)
    al = jnp.exp2(m0 - m)
    return normed(l0 * al + l, acc0 * al + acc)


def far_half(icy, q, kv, m, l, acc, put, c, half):
    @pl.when(icy == 0)
    def _():
        put(0, normed(l(0), acc(0)))
        put(1, fold(q(1), [kv(0, 0), kv(0, 1)], [kv(1, 0), kv(1, 1)], m(1), l(1), acc(1), c))

    @pl.when(icy != 0)
    def _():
        for part in range(2):
            put(part, fold(q(part), [kv(0, 0)], [kv(1, 0)], m(part), l(part), acc(part), c))


def main_kernel(ncx, scale, q_hbm, k_hbm, v_hbm,
                o_ref, qz, kvz, mz, lz, accz,
                q_s, kv_s, kin, f32s, bias_s, m_s, l_s, acc_s,
                q_sem, in_sem, ss, rs):
    nk, rows, rep, hd = q_s.shape
    c_rows = rows // 2
    half = c_rows * rep
    icy, icx = lax.axis_index('cy'), lax.axis_index('cx')
    dp = lax.axis_index('dp')
    me = icy * ncx + icx
    c = scale * LOG2E

    def dev(mask):
        t = me ^ mask
        return (dp, t // ncx, t % ncx)

    bar = pltpu.get_barrier_semaphore()
    for mask in (SIB, X, Y):
        pl.semaphore_signal(bar, inc=1, device_id=dev(mask), device_id_type=MESH)

    kcp = pltpu.make_async_copy(k_hbm, kin.at[0], in_sem.at[0])
    vcp = pltpu.make_async_copy(v_hbm, kin.at[1], in_sem.at[1])
    kcp.start()
    vcp.start()

    def qcopy(g):
        return pltpu.make_async_copy(q_hbm.at[:, g], q_s.at[g], q_sem.at[g])

    for g in range(nk):
        qcopy(g).start()

    def rcopy(kind, g, src, dst, mask):
        return pltpu.make_async_remote_copy(
            src_ref=src, dst_ref=dst, send_sem=ss.at[kind, g], recv_sem=rs.at[kind, g],
            device_id=dev(mask), device_id_type=MESH)

    def own(g, kind, mask):
        return rcopy(kind, g, kv_s.at[g, :, :, 0], kv_s.at[g, :, :, mask], mask)

    def own_sib(g):
        return own(g, 0, SIB)

    def own_x(g):
        return own(g, 1, X)

    def own_y(g):
        return own(g, 2, Y)

    def fwd_v(g):
        return rcopy(3, g, kv_s.at[g, 1, :, X], kv_s.at[g, 1, :, X ^ Y], Y)

    def fwd_k(g):
        return rcopy(4, g, kv_s.at[g, 0, :, Y], kv_s.at[g, 0, :, X ^ Y], X)

    def sib_x(g):
        return rcopy(5, g, kv_s.at[g, :, :, X], kv_s.at[g, :, :, X ^ SIB], SIB)

    def sib_y(g):
        return rcopy(6, g, kv_s.at[g, :, :, Y], kv_s.at[g, :, :, Y ^ SIB], SIB)

    def sib_d(g):
        return rcopy(7, g, kv_s.at[g, :, :, X ^ Y], kv_s.at[g, :, :, X ^ Y ^ SIB], SIB)

    kcp.wait()
    vcp.wait()
    for i in range(2):
        f32s[i] = kin[i].astype(jnp.float32).reshape(rows * nk, hd)

    def head_major(g):
        for i in range(2):
            x = f32s[i, pl.ds(g, rows, stride=nk), :].astype(jnp.bfloat16)
            kv_s[g, i, 0, 0] = x[:c_rows]
            kv_s[g, i, 1, 0] = x[c_rows:]

    head_major(0)
    head_major(1)
    pl.semaphore_wait(bar, 3)
    for g in range(nk):
        if g < LEAD:
            own_x(g).start()
            own_y(g).start()
        own_sib(g).start()
        if g + 2 < nk:
            head_major(g + 2)

    shape = (half, 4 * c_rows)
    qi = lax.broadcasted_iota(jnp.int32, shape, 0) // rep
    col = lax.broadcasted_iota(jnp.int32, shape, 1)
    slot = col // c_rows
    diag = (slot == 0) & (col % c_rows <= qi)
    e = slot ^ me
    bias_s[0] = jnp.where(diag | (e < me), 0.0, NEG)
    bias_s[1] = jnp.where(diag | (e > me), 0.0, NEG)

    def keys(g, i, fs, far):
        return kv_s[g, i, fs, pl.ds(4 * far, 4)].reshape(4 * c_rows, hd)

    def q_rows(g, part):
        return q_s[g, pl.ds(part * c_rows, c_rows)].reshape(half, hd)

    def part_rows(part):
        return pl.ds(part * half, half)

    def near(g, m_ref, l_ref, acc_ref):
        kf, ks = keys(g, 0, 0, 0), keys(g, 0, 1, 0)
        vf, vs = keys(g, 1, 0, 0), keys(g, 1, 1, 0)
        q = q_s[g].reshape(2 * half, hd)
        sf = scores(q, kf)
        s_a = [sf[:half] + bias_s[0]]
        s_b = [sf[half:], scores(q[half:], ks) + bias_s[1]]
        for part, sp, vv in ((0, s_a, [vf]), (1, s_b, [vf, vs])):
            m = jnp.broadcast_to(row_max(sp) * c, (half, hd))
            l, acc = weigh(sp, vv, m, c)
            m_ref[part_rows(part)] = m
            l_ref[part_rows(part)] = l
            acc_ref[part_rows(part)] = acc

    def far(g):
        def put(part, o):
            o_ref[g, pl.ds(part * c_rows, c_rows)] = o.reshape(c_rows, rep, hd)

        far_half(icy, functools.partial(q_rows, g), lambda i, fs: keys(g, i, fs, 1),
                 lambda p: m_s[g, part_rows(p)], lambda p: l_s[g, part_rows(p)],
                 lambda p: acc_s[g, part_rows(p)], put, c, half)

    def take_own(g):
        own_x(g).wait_recv()
        fwd_v(g).start()
        sib_x(g).start()
        own_y(g).wait_recv()
        fwd_k(g).start()
        sib_y(g).start()

    def take_diag(g):
        fwd_v(g).wait_recv()
        fwd_k(g).wait_recv()
        sib_d(g).start()

    def near_step(g):
        qcopy(g).wait()
        own_sib(g).wait_recv()
        sib_x(g).wait_recv()
        near(g, m_s.at[g], l_s.at[g], acc_s.at[g])

    def far_step(g):
        sib_y(g).wait_recv()
        sib_d(g).wait_recv()
        far(g)

    last = nk - 1

    def early(g, _):
        take_own(g)

        @pl.when(g + LEAD < nk)
        def _():
            own_x(g + LEAD).start()
            own_y(g + LEAD).start()

        @pl.when(g > 0)
        def _():
            near_step(g - 1)
        return 0

    lax.fori_loop(0, LEAD, early, 0)

    def middle(g, _):
        take_own(g)
        take_diag(g - LEAD)
        near_step(g - 1)

        @pl.when(g > LEAD)
        def _():
            far_step(g - LEAD - 1)
        return 0

    lax.fori_loop(LEAD, nk, middle, 0)

    take_diag(nk - LEAD)
    qcopy(last).wait()
    own_sib(last).wait_recv()
    sib_x(last).wait_recv()
    near(last, mz, lz, accz)
    qz[...] = q_s[last].reshape(2 * half, hd)
    far_step(last - LEAD)

    def late(g, _):
        take_diag(g - LEAD)
        far_step(g - LEAD - 1)
        return 0

    lax.fori_loop(nk + 1, nk + LEAD, late, 0)

    def drain(g, _):
        for f in (own_sib, own_x, own_y, fwd_v, fwd_k, sib_x, sib_y):
            f(g).wait_send()
        return 0

    lax.fori_loop(0, nk, drain, 0)
    sib_y(last).wait_recv()
    for g in range(nk):
        sib_d(g).wait_send()
    sib_d(last).wait_recv()
    for i in range(2):
        for fs in range(2):
            kvz[i, fs] = keys(last, i, fs, 1)


def last_kernel(rows, o_ref, qz, kvz, mz, lz, accz, out, oz, sem):
    nk, _, rep, hd = o_ref.shape
    c_rows = rows // 2
    half = c_rows * rep
    cps = [pltpu.make_async_copy(o_ref.at[g], out.at[:, g], sem.at[g]) for g in range(nk - 1)]
    for cp in cps:
        cp.start()

    def part_rows(part):
        return pl.ds(part * half, half)

    def put(part, o):
        oz[pl.ds(part * c_rows, c_rows)] = o.reshape(c_rows, rep, hd)

    far_half(lax.axis_index('cy'), lambda p: qz[part_rows(p)], lambda i, fs: kvz[i, fs],
             lambda p: mz[part_rows(p)], lambda p: lz[part_rows(p)], lambda p: accz[part_rows(p)],
             put, hd ** -0.5 * LOG2E, half)
    cp = pltpu.make_async_copy(oz, out.at[:, nk - 1], sem.at[nk - 1])
    cp.start()
    for cp_ in cps:
        cp_.wait()
    cp.wait()


def solution(mesh):
    ncx = mesh.shape['cx']
    spec = P(('dp', 'cy', 'cx'))
    bf16, f32 = jnp.bfloat16, jnp.float32

    def local(q, k, v):
        t, nh, hd = q.shape
        nk = k.shape[1]
        rep = nh // nk
        n = mesh.shape['cy'] * ncx
        c = t // 2
        scale = hd ** -0.5
        q4 = q.reshape(t, nk, rep, hd)
        hbm = pl.BlockSpec(memory_space=pltpu.HBM)
        vmem = pl.BlockSpec(memory_space=pltpu.VMEM)
        outs = pl.pallas_call(
            functools.partial(main_kernel, ncx, scale),
            out_shape=(
                pltpu.VMEM((nk, t, rep, hd), bf16),
                pltpu.VMEM((t * rep, hd), bf16),
                pltpu.VMEM((2, 2, n * c // 2, hd), bf16),
                pltpu.VMEM((t * rep, hd), f32),
                pltpu.VMEM((t * rep, hd), f32),
                pltpu.VMEM((t * rep, hd), f32),
            ),
            in_specs=[hbm] * 3,
            out_specs=(vmem,) * 6,
            scratch_shapes=[
                pltpu.VMEM((nk, t, rep, hd), bf16),
                pltpu.VMEM((nk, 2, 2, n, c, hd), bf16),
                pltpu.VMEM((2, t, nk, hd), bf16),
                pltpu.VMEM((2, t * nk, hd), f32),
                pltpu.VMEM((2, c * rep, 4 * c), f32),
                pltpu.VMEM((nk - 1, t * rep, hd), f32),
                pltpu.VMEM((nk - 1, t * rep, hd), f32),
                pltpu.VMEM((nk - 1, t * rep, hd), f32),
                pltpu.SemaphoreType.DMA((nk,)),
                pltpu.SemaphoreType.DMA((2,)),
                pltpu.SemaphoreType.DMA((8, nk)),
                pltpu.SemaphoreType.DMA((8, nk)),
            ],
            compiler_params=pltpu.CompilerParams(
                collective_id=0, has_side_effects=True, vmem_limit_bytes=40 * 2**20),
        )(*(pltpu.with_memory_space_constraint(x, pltpu.HBM) for x in (q4, k, v)))
        outs = [pltpu.with_memory_space_constraint(x, pltpu.VMEM) for x in outs]
        out = pl.pallas_call(
            functools.partial(last_kernel, t),
            out_shape=jax.ShapeDtypeStruct((t, nk, rep, hd), bf16),
            in_specs=[vmem] * 6,
            out_specs=hbm,
            scratch_shapes=[pltpu.VMEM((t, rep, hd), bf16), pltpu.SemaphoreType.DMA((nk,))],
            compiler_params=pltpu.CompilerParams(vmem_limit_bytes=16 * 2**20),
        )(*outs)
        return out.reshape(t, nh, hd)

    return jax.shard_map(local, mesh=mesh, in_specs=(spec, spec, spec), out_specs=spec, check_vma=False)
```

time: 45.8 us -> 29.1 us (0.64)
  the two profiles are of different devices: /device:TPU:4 before, /device:TPU:0 now
where the time goes in v2:
time: 29.1 us; the launch traced here: 29 us
  Pallas kernels  29 us (100%)
    pallas_call x1, Pallas kernels, local(): pl.pallas_call(functools.partial(main_kernel, ncx, scale), out_shape=(plt...  27.6 us
    pallas_call x1, Pallas kernels, local(): pl.pallas_call(functools.partial(last_kernel, t), out_shape=jax.ShapeDtyp...  1.41 us

profile of v2, /device:TPU:0, one launch (start us, length us, event | category | flops | bytes accessed | tf_op | source)
XLA Modules:
  0.0 29.0 jit_solution(3829582132589938874)
XLA Ops:
  0.0 27.6 %shard_map.37 = (bf16[8,128,8,128]{3,2,1,0:T(8,128)(2,1)S(1)}, bf16[1024,128]{1,0:T(8,128)(2,1)S(1)}, bf16[2,2,256,128]{3,2,1,0:T(8,128)(2,1)S(1)}, f32[1024,128...) custom-call(bf16[128,8,8,128]{3,2,1,0:T(8,128)(2,1)} %bitcast.2, bf16[128,8,128]{2,1,0:T(8,128)(2,1)} %k_hbm.1, ...), custom_call_target="tpu_custom_call" | custom-call | tf_op jit(solution)/shard_map/pallas_call | solution.py:321
  27.6 1.4 %shard_map.38 = bf16[128,8,8,128]{3,2,1,0:T(8,128)(2,1)} custom-call(bf16[8,128,8,128]{3,2,1,0:T(8,128)(2,1)S(1)} %get-tuple-element.11.o_ref, bf16[1024,128]{1,0:T(8,128)(2,1)S(1)} %get-tuple-element.12.qz, bf16[2,2,256,128]{3,2,1,0:T(8,128)(2,1)S(1)} %get-tuple-element.13.kvz, f32[1024,128]{1,0:T(8,128)S(1)} %get-tuple-element.14.mz, ...), custom_call_target="tpu_custom_call" | custom-call | tf_op jit(solution)/shard_map/pallas_call | solution.py:351

commit v3 on v2

--- a/solution.py
+++ b/solution.py
@@ -74,7 +74,7 @@
 def main_kernel(ncx, scale, q_hbm, k_hbm, v_hbm,
                 o_ref, qz, kvz, mz, lz, accz,
                 q_s, kv_s, kin, f32s, bias_s, m_s, l_s, acc_s,
-                q_sem, in_sem, ss, rs):
+                in_sem, ss, rs):
     nk, rows, rep, hd = q_s.shape
     c_rows = rows // 2
     half = c_rows * rep
@@ -96,46 +96,45 @@
     kcp.start()
     vcp.start()
 
-    def qcopy(g):
-        return pltpu.make_async_copy(q_hbm.at[:, g], q_s.at[g], q_sem.at[g])
-
-    for g in range(nk):
-        qcopy(g).start()
-
-    def rcopy(kind, g, src, dst, mask):
+    def rcopy(kind, arrival, g, src, dst, mask):
         return pltpu.make_async_remote_copy(
-            src_ref=src, dst_ref=dst, send_sem=ss.at[kind, g], recv_sem=rs.at[kind, g],
+            src_ref=src, dst_ref=dst, send_sem=ss.at[kind], recv_sem=rs.at[arrival, g],
             device_id=dev(mask), device_id_type=MESH)
 
-    def own(g, kind, mask):
-        return rcopy(kind, g, kv_s.at[g, :, :, 0], kv_s.at[g, :, :, mask], mask)
+    def slot(g, mask, n=1):
+        return kv_s.at[g, :, :, pl.ds(mask, n)]
 
     def own_sib(g):
-        return own(g, 0, SIB)
+        return rcopy(0, 1, g, slot(g, 0), slot(g, SIB), SIB)
 
     def own_x(g):
-        return own(g, 1, X)
+        return rcopy(1, 0, g, slot(g, 0), slot(g, X), X)
 
     def own_y(g):
-        return own(g, 2, Y)
+        return rcopy(2, 0, g, slot(g, 0), slot(g, Y), Y)
 
     def fwd_v(g):
-        return rcopy(3, g, kv_s.at[g, 1, :, X], kv_s.at[g, 1, :, X ^ Y], Y)
+        return rcopy(3, 2, g, kv_s.at[g, 1, :, X], kv_s.at[g, 1, :, X ^ Y], Y)
 
     def fwd_k(g):
-        return rcopy(4, g, kv_s.at[g, 0, :, Y], kv_s.at[g, 0, :, X ^ Y], X)
+        return rcopy(4, 2, g, kv_s.at[g, 0, :, Y], kv_s.at[g, 0, :, X ^ Y], X)
 
     def sib_x(g):
-        return rcopy(5, g, kv_s.at[g, :, :, X], kv_s.at[g, :, :, X ^ SIB], SIB)
+        return rcopy(5, 1, g, slot(g, X), slot(g, X ^ SIB), SIB)
 
     def sib_y(g):
-        return rcopy(6, g, kv_s.at[g, :, :, Y], kv_s.at[g, :, :, Y ^ SIB], SIB)
+        return rcopy(6, 3, g, slot(g, Y), slot(g, Y ^ SIB), SIB)
 
     def sib_d(g):
-        return rcopy(7, g, kv_s.at[g, :, :, X ^ Y], kv_s.at[g, :, :, X ^ Y ^ SIB], SIB)
+        return rcopy(7, 3, g, slot(g, X ^ Y), slot(g, X ^ Y ^ SIB), SIB)
+
+    def arrived(arrival, g, n):
+        rcopy(0, arrival, g, slot(g, 0, n), slot(g, 0, n), SIB).wait_recv()
 
     kcp.wait()
     vcp.wait()
+    for g in range(nk):
+        pltpu.make_async_copy(q_hbm.at[:, g], q_s.at[g], in_sem.at[2]).start()
     for i in range(2):
         f32s[i] = kin[i].astype(jnp.float32).reshape(rows * nk, hd)
 
@@ -152,16 +151,17 @@
         if g < LEAD:
             own_x(g).start()
             own_y(g).start()
-        own_sib(g).start()
+        if g < 2:
+            own_sib(g).start()
         if g + 2 < nk:
             head_major(g + 2)
 
     shape = (half, 4 * c_rows)
     qi = lax.broadcasted_iota(jnp.int32, shape, 0) // rep
     col = lax.broadcasted_iota(jnp.int32, shape, 1)
-    slot = col // c_rows
-    diag = (slot == 0) & (col % c_rows <= qi)
-    e = slot ^ me
+    at = col // c_rows
+    diag = (at == 0) & (col % c_rows <= qi)
+    e = at ^ me
     bias_s[0] = jnp.where(diag | (e < me), 0.0, NEG)
     bias_s[1] = jnp.where(diag | (e > me), 0.0, NEG)
 
@@ -197,83 +197,84 @@
                  lambda p: acc_s[g, part_rows(p)], put, c, half)
 
     def take_own(g):
-        own_x(g).wait_recv()
+        arrived(0, g, 2)
         fwd_v(g).start()
+        fwd_k(g).start()
         sib_x(g).start()
-        own_y(g).wait_recv()
-        fwd_k(g).start()
         sib_y(g).start()
 
     def take_diag(g):
-        fwd_v(g).wait_recv()
-        fwd_k(g).wait_recv()
+        arrived(2, g, 1)
         sib_d(g).start()
 
     def near_step(g):
-        qcopy(g).wait()
-        own_sib(g).wait_recv()
-        sib_x(g).wait_recv()
+        arrived(1, g, 2)
         near(g, m_s.at[g], l_s.at[g], acc_s.at[g])
 
     def far_step(g):
-        sib_y(g).wait_recv()
-        sib_d(g).wait_recv()
+        arrived(3, g, 2)
         far(g)
 
     last = nk - 1
 
     def early(g, _):
         take_own(g)
+        own_x(g + LEAD).start()
+        own_y(g + LEAD).start()
+        own_sib(g + 2).start()
+
+        @pl.when(g == 1)
+        def _():
+            pltpu.make_async_copy(o_ref, q_s, in_sem.at[2]).wait()
+
+        @pl.when(g > 0)
+        def _():
+            near_step(g - 1)
+        return 0
+
+    lax.fori_loop(0, LEAD - 1, early, 0)
+
+    def middle(g, _):
+        take_own(g)
 
         @pl.when(g + LEAD < nk)
         def _():
             own_x(g + LEAD).start()
             own_y(g + LEAD).start()
 
-        @pl.when(g > 0)
-        def _():
-            near_step(g - 1)
+        @pl.when(g + 2 < nk)
+        def _():
+            own_sib(g + 2).start()
+        near_step(g - 1)
+        take_diag(g - LEAD + 1)
+
+        @pl.when(g >= LEAD)
+        def _():
+            far_step(g - LEAD)
         return 0
 
-    lax.fori_loop(0, LEAD, early, 0)
-
-    def middle(g, _):
-        take_own(g)
-        take_diag(g - LEAD)
-        near_step(g - 1)
-
-        @pl.when(g > LEAD)
-        def _():
-            far_step(g - LEAD - 1)
-        return 0
-
-    lax.fori_loop(LEAD, nk, middle, 0)
-
-    take_diag(nk - LEAD)
-    qcopy(last).wait()
-    own_sib(last).wait_recv()
-    sib_x(last).wait_recv()
+    lax.fori_loop(LEAD - 1, nk, middle, 0)
+
+    arrived(1, last, 2)
     near(last, mz, lz, accz)
     qz[...] = q_s[last].reshape(2 * half, hd)
-    far_step(last - LEAD)
+    take_diag(nk - LEAD + 1)
+    far_step(nk - LEAD)
+    take_diag(nk - LEAD + 2)
+    take_diag(nk - LEAD + 3)
 
     def late(g, _):
-        take_diag(g - LEAD)
-        far_step(g - LEAD - 1)
+        far_step(g)
         return 0
 
-    lax.fori_loop(nk + 1, nk + LEAD, late, 0)
-
-    def drain(g, _):
-        for f in (own_sib, own_x, own_y, fwd_v, fwd_k, sib_x, sib_y):
-            f(g).wait_send()
-        return 0
-
-    lax.fori_loop(0, nk, drain, 0)
-    sib_y(last).wait_recv()
-    for g in range(nk):
-        sib_d(g).wait_send()
-    sib_d(last).wait_recv()
+    lax.fori_loop(nk - LEAD + 1, last, late, 0)
+    whole = kv_s.at[:, :, :, 0]
+    for kind in range(8):
+        ref = kv_s.at[:, 0, :, 0] if kind in (3, 4) else whole
+        pltpu.make_async_remote_copy(
+            src_ref=ref, dst_ref=ref, send_sem=ss.at[kind], recv_sem=rs.at[0, 0],
+            device_id=dev(SIB), device_id_type=MESH).wait_send()
+    arrived(3, last, 2)
     for i in range(2):
         for fs in range(2):
             kvz[i, fs] = keys(last, i, fs, 1)
@@ -339,10 +340,9 @@
                 pltpu.VMEM((nk - 1, t * rep, hd), f32),
                 pltpu.VMEM((nk - 1, t * rep, hd), f32),
                 pltpu.VMEM((nk - 1, t * rep, hd), f32),
-                pltpu.SemaphoreType.DMA((nk,)),
-                pltpu.SemaphoreType.DMA((2,)),
-                pltpu.SemaphoreType.DMA((8, nk)),
-                pltpu.SemaphoreType.DMA((8, nk)),
+                pltpu.SemaphoreType.DMA((3,)),
+                pltpu.SemaphoreType.DMA((8,)),
+                pltpu.SemaphoreType.DMA((4, nk)),
             ],
             compiler_params=pltpu.CompilerParams(
                 collective_id=0, has_side_effects=True, vmem_limit_bytes=40 * 2**20),

time: 29.1 us -> 26.7 us (0.918)
  Pallas kernels: 29 us -> 26.5 us
    pallas_call x1, Pallas kernels: 27.6 us -> 25.1 us  [local(): pl.pallas_call(functools.partial(main_kernel, ncx, scale), out_shape=(plt...]
where the time goes in v3:
time: 26.7 us; the launch traced here: 26.6 us
  Pallas kernels  26.5 us (99%)
    pallas_call x1, Pallas kernels, local(): pl.pallas_call(functools.partial(main_kernel, ncx, scale), out_shape=(plt...  25.1 us
    pallas_call x1, Pallas kernels, local(): pl.pallas_call(functools.partial(last_kernel, t), out_shape=jax.ShapeDtyp...  1.41 us

profile of v3, /device:TPU:0, one launch (start us, length us, event | category | flops | bytes accessed | tf_op | source)
XLA Modules:
  0.0 26.6 jit_solution(4813936078515931589)
XLA Ops:
  0.0 25.1 %shard_map.37 = (bf16[8,128,8,128]{3,2,1,0:T(8,128)(2,1)S(1)}, bf16[1024,128]{1,0:T(8,128)(2,1)S(1)}, bf16[2,2,256,128]{3,2,1,0:T(8,128)(2,1)S(1)}, f32[1024,128...) custom-call(bf16[128,8,8,128]{3,2,1,0:T(8,128)(2,1)} %bitcast.2, bf16[128,8,128]{2,1,0:T(8,128)(2,1)} %k_hbm.1, ...), custom_call_target="tpu_custom_call" | custom-call | tf_op jit(solution)/shard_map/pallas_call | solution.py:322
  25.1 1.4 %shard_map.38 = bf16[128,8,8,128]{3,2,1,0:T(8,128)(2,1)} custom-call(bf16[8,128,8,128]{3,2,1,0:T(8,128)(2,1)S(1)} %get-tuple-element.11.o_ref, bf16[1024,128]{1,0:T(8,128)(2,1)S(1)} %get-tuple-element.12.qz, bf16[2,2,256,128]{3,2,1,0:T(8,128)(2,1)S(1)} %get-tuple-element.13.kvz, f32[1024,128]{1,0:T(8,128)S(1)} %get-tuple-element.14.mz, ...), custom_call_target="tpu_custom_call" | custom-call | tf_op jit(solution)/shard_map/pallas_call | solution.py:351

commit v4 on v3

--- a/solution.py
+++ b/solution.py
@@ -14,7 +14,8 @@
 LANES = 128
 
 SIB, X, Y = 1, 2, 4
-LEAD = 4
+LOADS = 4
+LEAD = 6
 
 
 def lane_blocks(s):
@@ -74,7 +75,7 @@
 def main_kernel(ncx, scale, q_hbm, k_hbm, v_hbm,
                 o_ref, qz, kvz, mz, lz, accz,
                 q_s, kv_s, kin, f32s, bias_s, m_s, l_s, acc_s,
-                in_sem, ss, rs):
+                in_sem, out_sem, rs):
     nk, rows, rep, hd = q_s.shape
     c_rows = rows // 2
     half = c_rows * rep
@@ -91,50 +92,50 @@
     for mask in (SIB, X, Y):
         pl.semaphore_signal(bar, inc=1, device_id=dev(mask), device_id_type=MESH)
 
-    kcp = pltpu.make_async_copy(k_hbm, kin.at[0], in_sem.at[0])
-    vcp = pltpu.make_async_copy(v_hbm, kin.at[1], in_sem.at[1])
-    kcp.start()
-    vcp.start()
-
-    def rcopy(kind, arrival, g, src, dst, mask):
+    part = rows // LOADS
+    for i in range(LOADS):
+        for j, ref in enumerate((k_hbm, v_hbm)):
+            sl = pl.ds(i * part, part)
+            pltpu.make_async_copy(ref.at[sl], kin.at[j, sl], in_sem.at[0]).start()
+
+    def rcopy(arrival, g, src, dst, mask):
         return pltpu.make_async_remote_copy(
-            src_ref=src, dst_ref=dst, send_sem=ss.at[kind], recv_sem=rs.at[arrival, g],
+            src_ref=src, dst_ref=dst, send_sem=out_sem, recv_sem=rs.at[arrival, g],
             device_id=dev(mask), device_id_type=MESH)
 
     def slot(g, mask, n=1):
         return kv_s.at[g, :, :, pl.ds(mask, n)]
 
     def own_sib(g):
-        return rcopy(0, 1, g, slot(g, 0), slot(g, SIB), SIB)
+        return rcopy(1, g, slot(g, 0), slot(g, SIB), SIB)
 
     def own_x(g):
-        return rcopy(1, 0, g, slot(g, 0), slot(g, X), X)
+        return rcopy(0, g, slot(g, 0), slot(g, X), X)
 
     def own_y(g):
-        return rcopy(2, 0, g, slot(g, 0), slot(g, Y), Y)
+        return rcopy(0, g, slot(g, 0), slot(g, Y), Y)
 
     def fwd_v(g):
-        return rcopy(3, 2, g, kv_s.at[g, 1, :, X], kv_s.at[g, 1, :, X ^ Y], Y)
+        return rcopy(2, g, kv_s.at[g, 1, :, X], kv_s.at[g, 1, :, X ^ Y], Y)
 
     def fwd_k(g):
-        return rcopy(4, 2, g, kv_s.at[g, 0, :, Y], kv_s.at[g, 0, :, X ^ Y], X)
+        return rcopy(2, g, kv_s.at[g, 0, :, Y], kv_s.at[g, 0, :, X ^ Y], X)
 
     def sib_x(g):
-        return rcopy(5, 1, g, slot(g, X), slot(g, X ^ SIB), SIB)
+        return rcopy(1, g, slot(g, X), slot(g, X ^ SIB), SIB)
 
     def sib_y(g):
-        return rcopy(6, 3, g, slot(g, Y), slot(g, Y ^ SIB), SIB)
+        return rcopy(3, g, slot(g, Y), slot(g, Y ^ SIB), SIB)
 
     def sib_d(g):
-        return rcopy(7, 3, g, slot(g, X ^ Y), slot(g, X ^ Y ^ SIB), SIB)
+        return rcopy(3, g, slot(g, X ^ Y), slot(g, X ^ Y ^ SIB), SIB)
 
     def arrived(arrival, g, n):
-        rcopy(0, arrival, g, slot(g, 0, n), slot(g, 0, n), SIB).wait_recv()
-
-    kcp.wait()
-    vcp.wait()
+        rcopy(arrival, g, slot(g, 0, n), slot(g, 0, n), SIB).wait_recv()
+
+    pltpu.make_async_copy(kin, kin, in_sem.at[0]).wait()
     for g in range(nk):
-        pltpu.make_async_copy(q_hbm.at[:, g], q_s.at[g], in_sem.at[2]).start()
+        pltpu.make_async_copy(q_hbm.at[:, g], q_s.at[g], in_sem.at[1]).start()
     for i in range(2):
         f32s[i] = kin[i].astype(jnp.float32).reshape(rows * nk, hd)
 
@@ -151,8 +152,7 @@
         if g < LEAD:
             own_x(g).start()
             own_y(g).start()
-        if g < 2:
-            own_sib(g).start()
+        own_sib(g).start()
         if g + 2 < nk:
             head_major(g + 2)
 
@@ -217,15 +217,19 @@
 
     last = nk - 1
 
+    def own_next(g):
+        @pl.when(g + LEAD < nk)
+        def _():
+            own_x(g + LEAD).start()
+            own_y(g + LEAD).start()
+
     def early(g, _):
         take_own(g)
-        own_x(g + LEAD).start()
-        own_y(g + LEAD).start()
-        own_sib(g + 2).start()
+        own_next(g)
 
         @pl.when(g == 1)
         def _():
-            pltpu.make_async_copy(o_ref, q_s, in_sem.at[2]).wait()
+            pltpu.make_async_copy(o_ref, q_s, in_sem.at[1]).wait()
 
         @pl.when(g > 0)
         def _():
@@ -236,15 +240,7 @@
 
     def middle(g, _):
         take_own(g)
-
-        @pl.when(g + LEAD < nk)
-        def _():
-            own_x(g + LEAD).start()
-            own_y(g + LEAD).start()
-
-        @pl.when(g + 2 < nk)
-        def _():
-            own_sib(g + 2).start()
+        own_next(g)
         near_step(g - 1)
         take_diag(g - LEAD + 1)
 
@@ -259,21 +255,19 @@
     near(last, mz, lz, accz)
     qz[...] = q_s[last].reshape(2 * half, hd)
     take_diag(nk - LEAD + 1)
-    far_step(nk - LEAD)
-    take_diag(nk - LEAD + 2)
-    take_diag(nk - LEAD + 3)
 
     def late(g, _):
+        @pl.when(g + 2 < nk)
+        def _():
+            take_diag(g + 2)
         far_step(g)
         return 0
 
-    lax.fori_loop(nk - LEAD + 1, last, late, 0)
-    whole = kv_s.at[:, :, :, 0]
-    for kind in range(8):
-        ref = kv_s.at[:, 0, :, 0] if kind in (3, 4) else whole
-        pltpu.make_async_remote_copy(
-            src_ref=ref, dst_ref=ref, send_sem=ss.at[kind], recv_sem=rs.at[0, 0],
-            device_id=dev(SIB), device_id_type=MESH).wait_send()
+    lax.fori_loop(nk - LEAD, last, late, 0)
+    ref = kv_s.at[:, :, :, pl.ds(0, 7)]
+    pltpu.make_async_remote_copy(
+        src_ref=ref, dst_ref=ref, send_sem=out_sem, recv_sem=rs.at[0, 0],
+        device_id=dev(SIB), device_id_type=MESH).wait_send()
     arrived(3, last, 2)
     for i in range(2):
         for fs in range(2):
@@ -340,8 +334,8 @@
                 pltpu.VMEM((nk - 1, t * rep, hd), f32),
                 pltpu.VMEM((nk - 1, t * rep, hd), f32),
                 pltpu.VMEM((nk - 1, t * rep, hd), f32),
-                pltpu.SemaphoreType.DMA((3,)),
-                pltpu.SemaphoreType.DMA((8,)),
+                pltpu.SemaphoreType.DMA((2,)),
+                pltpu.SemaphoreType.DMA,
                 pltpu.SemaphoreType.DMA((4, nk)),
             ],
             compiler_params=pltpu.CompilerParams(

time: 26.7 us -> 26.5 us (level)
  no operation moved by 1% of the time
where the time goes in v4:
time: 26.5 us; the launch traced here: 26.4 us
  Pallas kernels  26.4 us (100%)
    pallas_call x1, Pallas kernels, local(): pl.pallas_call(functools.partial(main_kernel, ncx, scale), out_shape=(plt...  25 us
    pallas_call x1, Pallas kernels, local(): pl.pallas_call(functools.partial(last_kernel, t), out_shape=jax.ShapeDtyp...  1.41 us

profile of v4, /device:TPU:0, one launch (start us, length us, event | category | flops | bytes accessed | tf_op | source)
XLA Modules:
  0.0 26.4 jit_solution(18056109203014408572)
XLA Ops:
  0.0 25.0 %shard_map.37 = (bf16[8,128,8,128]{3,2,1,0:T(8,128)(2,1)S(1)}, bf16[1024,128]{1,0:T(8,128)(2,1)S(1)}, bf16[2,2,256,128]{3,2,1,0:T(8,128)(2,1)S(1)}, f32[1024,128...) custom-call(bf16[128,8,8,128]{3,2,1,0:T(8,128)(2,1)} %bitcast.2, bf16[128,8,128]{2,1,0:T(8,128)(2,1)} %k_hbm.1, ...), custom_call_target="tpu_custom_call" | custom-call | tf_op jit(solution)/shard_map/pallas_call | solution.py:316
  25.0 1.4 %shard_map.38 = bf16[128,8,8,128]{3,2,1,0:T(8,128)(2,1)} custom-call(bf16[8,128,8,128]{3,2,1,0:T(8,128)(2,1)S(1)} %get-tuple-element.11.o_ref, bf16[1024,128]{1,0:T(8,128)(2,1)S(1)} %get-tuple-element.12.qz, bf16[2,2,256,128]{3,2,1,0:T(8,128)(2,1)S(1)} %get-tuple-element.13.kvz, f32[1024,128]{1,0:T(8,128)S(1)} %get-tuple-element.14.mz, ...), custom_call_target="tpu_custom_call" | custom-call | tf_op jit(solution)/shard_map/pallas_call | solution.py:345

commit v5 on v4

v5 whole, which is shorter than its diff:
```python
import functools

import jax
import jax.numpy as jnp
from jax import lax
from jax.experimental import pallas as pl
from jax.experimental.pallas import tpu as pltpu
from jax.sharding import PartitionSpec as P

NEG = -1.0e30
LOG2E = 1.4426950408889634
MESH = pl.DeviceIdType.MESH
NT = (((1,), (1,)), ((), ()))
LANES = 128

SIB, X, Y = 1, 2, 4
LOADS = 4
LEAD = 6


def lane_blocks(s):
    return [s[:, i:i + LANES] for i in range(0, s.shape[1], LANES)]


def tree(f, xs):
    xs = list(xs)
    while len(xs) > 1:
        xs = [f(*xs[i:i + 2]) if i + 1 < len(xs) else xs[i] for i in range(0, len(xs), 2)]
    return xs[0]


def scores(q, k):
    return lax.dot_general(q, k, NT, preferred_element_type=jnp.float32)


def row_max(ss):
    return jnp.max(tree(jnp.maximum, [b for s in ss for b in lane_blocks(s)]), axis=-1, keepdims=True)


def weigh(ss, vals, m, c):
    ls, acc = [], None
    for s, v in zip(ss, vals):
        ps = [jnp.exp2(b * c - m) for b in lane_blocks(s)]
        ls += ps
        p = jnp.concatenate([b.astype(jnp.bfloat16) for b in ps], axis=1)
        pv = jnp.dot(p, v, preferred_element_type=jnp.float32)
        acc = pv if acc is None else acc + pv
    return tree(jnp.add, ls), acc


def start_state(ss, vals, c):
    m = jnp.broadcast_to(row_max(ss) * c, (ss[0].shape[0], LANES))
    return (m,) + weigh(ss, vals, m, c)


def fold(state, q, kk, vv, c):
    m0, l0, acc0 = state
    ss = [scores(q, k) for k in kk]
    m = jnp.maximum(m0, row_max(ss) * c)
    l, acc = weigh(ss, vv, m, c)
    al = jnp.exp2(m0 - m)
    return m, l0 * al + l, acc0 * al + acc


class Head:
    def __init__(self, q, kv, m, l, acc):
        self.q, self.kv, self.state = q, kv, (m, l, acc)
        self.t, self.rep, self.hd = q.shape
        self.half = self.t // 2 * self.rep

    def rows(self, part):
        n = self.t // 2
        return self.q[pl.ds(part * n, n)].reshape(self.half, self.hd)

    def both(self, i, p):
        return self.kv[i, p].reshape(2 * self.t, self.hd)

    def first(self, i, p):
        return self.kv[i, p, 0].reshape(self.t, self.hd)

    def load(self, part):
        return tuple(r[pl.ds(part * self.half, self.half)] for r in self.state)

    def save(self, part, state):
        for r, x in zip(self.state, state):
            r[pl.ds(part * self.half, self.half)] = x

    def fold(self, part, keys, c):
        return fold(self.load(part), self.rows(part), keys(0), keys(1), c)

    def normed(self, state):
        _, l, acc = state
        o = (acc * (1.0 / jnp.sum(l, axis=-1, keepdims=True))).astype(jnp.bfloat16)
        return o.reshape(self.t // 2, self.rep, self.hd)

    def far(self, cy, put, c):
        if cy == 0:
            put(1, self.normed(self.fold(1, lambda i: [self.both(i, 2), self.both(i, 3)], c)))
        else:
            for part in range(2):
                keys = lambda i: [jnp.concatenate([self.first(i, 2), self.first(i, 3)], axis=0)]
                put(part, self.normed(self.fold(part, keys, c)))


def main_kernel(ncx, scale, q_hbm, k_hbm, v_hbm,
                o_ref, q_s, kv_s, m_s, l_s, acc_s,
                kin, f32s, bias_s, in_sem, out_sem, rs):
    nk, rows, rep, hd = q_s.shape
    c_rows = rows // 2
    half = c_rows * rep
    icy, icx = lax.axis_index('cy'), lax.axis_index('cx')
    dp = lax.axis_index('dp')
    me = icy * ncx + icx
    c = scale * LOG2E

    def dev(mask):
        t = me ^ mask
        return (dp, t // ncx, t % ncx)

    bar = pltpu.get_barrier_semaphore()
    for mask in (SIB, X, Y):
        pl.semaphore_signal(bar, inc=1, device_id=dev(mask), device_id_type=MESH)

    part = rows // LOADS
    for i in range(LOADS):
        for j, ref in enumerate((k_hbm, v_hbm)):
            sl = pl.ds(i * part, part)
            pltpu.make_async_copy(ref.at[sl], kin.at[j, sl], in_sem.at[0]).start()

    def rcopy(arrival, g, src, dst, mask):
        return pltpu.make_async_remote_copy(
            src_ref=src, dst_ref=dst, send_sem=out_sem, recv_sem=rs.at[arrival, g],
            device_id=dev(mask), device_id_type=MESH)

    def slot(g, mask, i=None):
        if i is None:
            return kv_s.at[g, :, mask // 2, :, mask % 2]
        return kv_s.at[g, i, mask // 2, :, mask % 2]

    def own_sib(g):
        return rcopy(4, g, slot(g, 0), slot(g, SIB), SIB)

    def own_x(g):
        return rcopy(0, g, slot(g, 0), slot(g, X), X)

    def own_y(g):
        return rcopy(0, g, slot(g, 0), slot(g, Y), Y)

    def fwd_v(g):
        return rcopy(2, g, slot(g, X, 1), slot(g, X ^ Y, 1), Y)

    def fwd_k(g):
        return rcopy(2, g, slot(g, Y, 0), slot(g, X ^ Y, 0), X)

    def sib_x(g):
        return rcopy(1, g, slot(g, X), slot(g, X ^ SIB), SIB)

    def sib_y(g):
        return rcopy(3, g, slot(g, Y), slot(g, Y ^ SIB), SIB)

    def sib_d(g):
        return rcopy(3, g, slot(g, X ^ Y), slot(g, X ^ Y ^ SIB), SIB)

    def arrived(arrival, g, n):
        ref = kv_s.at[g, :, 0] if n == 2 else slot(g, 0)
        rcopy(arrival, g, ref, ref, SIB).wait_recv()

    pltpu.make_async_copy(kin, kin, in_sem.at[0]).wait()
    for g in range(nk):
        pltpu.make_async_copy(q_hbm.at[:, g], q_s.at[g], in_sem.at[1]).start()
    for i in range(2):
        f32s[i] = kin[i].astype(jnp.float32).reshape(rows * nk, hd)

    def head_major(g):
        for i in range(2):
            x = f32s[i, pl.ds(g, rows, stride=nk), :].astype(jnp.bfloat16)
            kv_s[g, i, 0, 0, 0] = x[:c_rows]
            kv_s[g, i, 0, 1, 0] = x[c_rows:]

    head_major(0)
    head_major(1)
    pl.semaphore_wait(bar, 3)
    for g in range(nk):
        if g < LEAD:
            own_x(g).start()
            own_y(g).start()
        own_sib(g).start()
        if g + 2 < nk:
            head_major(g + 2)

    shape = (half, 2 * c_rows)
    qi = lax.broadcasted_iota(jnp.int32, shape, 0) // rep
    col = lax.broadcasted_iota(jnp.int32, shape, 1)
    at = col // c_rows
    diag = (at == 0) & (col % c_rows <= qi)
    e = at ^ me
    bias_s[0] = jnp.where(diag | (e < me), 0.0, NEG)
    bias_s[1] = jnp.where(diag | (e > me), 0.0, NEG)

    def head(g):
        return Head(q_s.at[g], kv_s.at[g], m_s.at[g], l_s.at[g], acc_s.at[g])

    def put_o(g, part, o):
        o_ref[g, pl.ds(part * c_rows, c_rows)] = o

    def local(g):
        h = head(g)
        s = scores(h.rows(0), h.first(0, 0)) + bias_s[0]
        st = start_state([s], [h.first(1, 0)], c)
        h.save(0, st)
        s = scores(h.rows(1), h.both(0, 0))
        s = jnp.concatenate([s[:, :2 * c_rows], s[:, 2 * c_rows:] + bias_s[1]], axis=1)
        h.save(1, start_state([s], [h.both(1, 0)], c))

    def side(g):
        h = head(g)

        @pl.when(icx < ncx // 2)
        def _():
            h.save(1, h.fold(1, lambda i: [h.both(i, 1)], c))

        @pl.when(icx >= ncx // 2)
        def _():
            for part in range(2):
                h.save(part, h.fold(part, lambda i: [h.first(i, 1)], c))

    def far(g):
        h = head(g)

        @pl.when(icy == 0)
        def _():
            put_o(g, 0, h.normed(h.load(0)))
            h.far(0, functools.partial(put_o, g), c)

        @pl.when(icy != 0)
        def _():
            h.far(1, functools.partial(put_o, g), c)

    def take_own(g):
        arrived(0, g, 2)
        fwd_v(g).start()
        fwd_k(g).start()
        sib_x(g).start()
        sib_y(g).start()

    def take_diag(g):
        arrived(2, g, 1)
        sib_d(g).start()

    last = nk - 1
    pltpu.make_async_copy(o_ref, q_s, in_sem.at[1]).wait()

    def local_step(g, _):
        arrived(4, g, 1)
        local(g)
        return 0

    lax.fori_loop(0, nk, local_step, 0)

    def side_step(g):
        arrived(1, g, 1)
        side(g)

    def far_step(g):
        arrived(3, g, 2)
        far(g)

    def step(g, _):
        take_own(g)

        @pl.when(g + LEAD < nk)
        def _():
            own_x(g + LEAD).start()
            own_y(g + LEAD).start()

        @pl.when(g > 0)
        def _():
            side_step(g - 1)

        @pl.when(g >= LEAD - 1)
        def _():
            take_diag(g - LEAD + 1)

        @pl.when(g >= LEAD)
        def _():
            far_step(g - LEAD)
        return 0

    lax.fori_loop(0, nk, step, 0)
    side_step(last)
    take_diag(nk - LEAD + 1)

    def late(g, _):
        @pl.when(g + 2 < nk)
        def _():
            take_diag(g + 2)
        far_step(g)
        return 0

    lax.fori_loop(nk - LEAD, last, late, 0)
    ref = kv_s.at[pl.ds(0, 7)]
    pltpu.make_async_remote_copy(
        src_ref=ref, dst_ref=ref, send_sem=out_sem, recv_sem=rs.at[0, 0],
        device_id=dev(SIB), device_id_type=MESH).wait_send()
    arrived(3, last, 2)


def last_kernel(o_ref, q_s, kv_s, m_s, l_s, acc_s, out, oz, sem):
    nk, t, rep, hd = o_ref.shape
    last = nk - 1
    cps = [pltpu.make_async_copy(o_ref.at[g], out.at[:, g], sem.at[g]) for g in range(last)]
    for cp in cps:
        cp.start()
    h = Head(*(r.at[last] for r in (q_s, kv_s, m_s, l_s, acc_s)))

    def put(part, o):
        oz[pl.ds(part * t // 2, t // 2)] = o

    for cy in (0, 1):
        @pl.when(lax.axis_index('cy') == cy)
        def _():
            if cy == 0:
                put(0, h.normed(h.load(0)))
            h.far(cy, put, hd ** -0.5 * LOG2E)

    cps.append(pltpu.make_async_copy(oz, out.at[:, last], sem.at[last]))
    cps[-1].start()
    for cp in cps:
        cp.wait()


def solution(mesh):
    ncx = mesh.shape['cx']
    spec = P(('dp', 'cy', 'cx'))
    bf16, f32 = jnp.bfloat16, jnp.float32

    def local(q, k, v):
        t, nh, hd = q.shape
        nk = k.shape[1]
        rep = nh // nk
        n = mesh.shape['cy'] * ncx
        c = t // 2
        scale = hd ** -0.5
        q4 = q.reshape(t, nk, rep, hd)
        hbm = pl.BlockSpec(memory_space=pltpu.HBM)
        vmem = pl.BlockSpec(memory_space=pltpu.VMEM)
        outs = pl.pallas_call(
            functools.partial(main_kernel, ncx, scale),
            out_shape=(
                pltpu.VMEM((nk, t, rep, hd), bf16),
                pltpu.VMEM((nk, t, rep, hd), bf16),
                pltpu.VMEM((nk, 2, n // 2, 2, 2, c, hd), bf16),
                pltpu.VMEM((nk, t * rep, hd), f32),
                pltpu.VMEM((nk, t * rep, hd), f32),
                pltpu.VMEM((nk, t * rep, hd), f32),
            ),
            in_specs=[hbm] * 3,
            out_specs=(vmem,) * 6,
            scratch_shapes=[
                pltpu.VMEM((2, t, nk, hd), bf16),
                pltpu.VMEM((2, t * nk, hd), f32),
                pltpu.VMEM((2, c * rep, 2 * c), f32),
                pltpu.SemaphoreType.DMA((2,)),
                pltpu.SemaphoreType.DMA,
                pltpu.SemaphoreType.DMA((5, nk)),
            ],
            compiler_params=pltpu.CompilerParams(
                collective_id=0, has_side_effects=True, vmem_limit_bytes=16 * 2**20),
        )(*(pltpu.with_memory_space_constraint(x, pltpu.HBM) for x in (q4, k, v)))
        outs = [pltpu.with_memory_space_constraint(x, pltpu.VMEM) for x in outs]
        out = pl.pallas_call(
            last_kernel,
            out_shape=jax.ShapeDtypeStruct((t, nk, rep, hd), bf16),
            in_specs=[vmem] * 6,
            out_specs=hbm,
            scratch_shapes=[pltpu.VMEM((t, rep, hd), bf16), pltpu.SemaphoreType.DMA((nk,))],
            compiler_params=pltpu.CompilerParams(vmem_limit_bytes=8 * 2**20),
        )(*outs)
        return out.reshape(t, nh, hd)

    return jax.shard_map(local, mesh=mesh, in_specs=(spec, spec, spec), out_specs=spec, check_vma=False)
```

time: 26.5 us -> 25.8 us (0.974)
  Pallas kernels: 26.4 us -> 25.7 us
    pallas_call x1, Pallas kernels: 25 us -> 24.3 us  [local(): pl.pallas_call(functools.partial(main_kernel, ncx, scale), out_shape=(plt...]
where the time goes in v5:
time: 25.8 us; the launch traced here: 25.7 us
  Pallas kernels  25.7 us (100%)
    pallas_call x1, Pallas kernels, local(): pl.pallas_call(functools.partial(main_kernel, ncx, scale), out_shape=(plt...  24.3 us
    pallas_call x1, Pallas kernels, local(): pl.pallas_call(last_kernel, out_shape=jax.ShapeDtypeStruct((t, nk, rep, h...  1.41 us

profile of v5, /device:TPU:0, one launch (start us, length us, event | category | flops | bytes accessed | tf_op | source)
XLA Modules:
  0.0 25.7 jit_solution(10240362024821157674)
XLA Ops:
  0.0 24.3 %shard_map.37 = (bf16[8,128,8,128]{3,2,1,0:T(8,128)(2,1)S(1)}, bf16[8,128,8,128]{3,2,1,0:T(8,128)(2,1)S(1)}, bf16[8,2,4,2,2,64,128]{6,5,4,3,2,1,0:T(8,128)(2,1)S...) custom-call(bf16[128,8,8,128]{3,2,1,0:T(8,128)(2,1)} %bitcast.2, ...), custom_call_target="tpu_custom_call" | custom-call | tf_op jit(solution)/shard_map/pallas_call | solution.py:347
  24.3 1.4 %shard_map.38 = bf16[128,8,8,128]{3,2,1,0:T(8,128)(2,1)} custom-call(bf16[8,128,8,128]{3,2,1,0:T(8,128)(2,1)S(1)} %get-tuple-element.11.o_ref, bf16[8,128,8,128]{3,2,1,0:T(8,128)(2,1)S(1)} %get-tuple-element.12.q_s, bf16[8,2,4,2,2,64,128]{6,5,4,3,2,1,0:T(8,128)(2,1)S(1)} %get-tuple-element.13.kv_s, f32[8,1024,128]{2,1,0:T(8,128)S(1)} %get-tuple-element.14.m_s, ...), custom_call_target="tpu_custom_call" | custom-call | tf_op jit(solution)/shard_map/pallas_call | solution.py:371
